TPU v7x, 512 devices: a whole 4x8x8 slice. The times are simulated.
512 devices in a mesh: replica: 32 (over y_hi, z), tp: 16 (over x, y_lo, core).
Axes of the slice: x: 4, y: 8 (y_hi: 4, y_lo: 2; y = y_hi * 2 + y_lo), z: 8, core: 2. Of those that a mesh axis runs over, the one named last changes fastest.
Arguments:
- hidden: bfloat16 [1536, 4, 8192], P('replica', None, 'tp'), may hold values from -6 to 6
- norm_gain: float32 [8192], replicated, may hold values from 0.5 to 1.5
- w_query: float32 [8192, 4096], P(('replica', 'tp')), may hold values from -0.0625 to 0.0625
- w_key: float32 [8192, 512], P(('replica', 'tp')), may hold values from -0.0625 to 0.0625
- w_value: float32 [8192, 512], P(('replica', 'tp')), may hold values from -0.0625 to 0.0625
- bias_query: float32 [4096], P('tp'), may hold values from -3 to 3
- bias_key: float32 [512], P('tp'), may hold values from -3 to 3
- bias_value: float32 [512], P('tp'), may hold values from -3 to 3
- key_pages: bfloat16 [8192, 4, 128, 128], P(('replica', 'tp')), may hold values from -256 to 256
- value_pages: bfloat16 [8192, 4, 128, 128], P(('replica', 'tp')), may hold values from -6 to 6
- kv_lengths: int32 [1536], P(('replica', 'tp')), may hold values from 1 to 1024, as said below
- page_table: int32 [1536, 8], P(('replica', 'tp')), may hold values from 0 to 15, as said below
Outputs:
- attended: bfloat16 [1536, 4, 4096], P(('replica', 'tp'))
Inputs may be any that keep to these rules, and one draw needn't show every extreme that they name: `kv_lengths`: on every device, one row has exactly 1024 cached tokens. `page_table`: page ids are local to the pool of 16 pages of the device that holds the row. The first ceil(kv_lengths / 128) entries of a row name its pages in order; no page serves two of those entries on one device; later entries are arbitrary pages of the pool.
All inputs are finite; a program needn't handle non-finite values.
Results may differ from a plain program's by a relative error of at most 0.04.
Values may be sent and summed in bfloat16 or wider, within the bound.
A program may use at most 128 MiB of HBM per device.

v0:
```python
import jax
import jax.numpy as jnp
from jax import lax
from jax.sharding import Mesh
from jax.sharding import PartitionSpec as P

HD = 128
HQ = 32
KVH = 4
PAGE = 128
MOSTP = 8
TP = ("tp_0", "tp_1", "tp_2")
REPLICA_TP = ("replica", "tp_0", "tp_1", "tp_2")


EPS = 1e-06
THETA = 1000000.0


def in_blocks(x, dim, devices):
    before, after = (x.shape[:dim], x.shape[dim + 1 :])
    return jnp.moveaxis(x.reshape(*before, devices, -1, *after), dim, 0)


def joined_along(pieces, dim):
    pieces = jnp.moveaxis(pieces, 0, dim)
    dims = pieces.shape
    return pieces.reshape(*dims[:dim], dims[dim] * dims[dim + 1], *dims[dim + 2 :])


def exchange_in_order(pieces, axes, order):
    inside = pieces.shape[1:]
    out = pieces.reshape(*(lax.axis_size(a) for a in axes), *inside)
    for k in order:
        out = lax.all_to_all(out, axes[k], k, k, tiled=True)
    return out.reshape(-1, *inside)


def two_step_exchange(x, groups, order, split_dim, concat_dim):
    devices = lax.axis_size(groups[0]) * lax.axis_size(groups[1])
    pieces = in_blocks(x, split_dim, devices)
    return joined_along(exchange_in_order(pieces, groups, order), concat_dim)


def side_by_side(arrays, axis, dim, along):
    widths = [a.shape[along] for a in arrays]
    both = jnp.concatenate(arrays, axis=along)
    out = lax.all_gather(both, axis, axis=dim, tiled=True)
    return tuple(jnp.split(out, [sum(widths[:k]) for k in range(1, len(widths))], axis=along))


def side_by_side_2(arrays, axis, split_dim, concat_dim, along):
    ends, at = ([], 0)
    for a in arrays[:-1]:
        at += a.shape[along]
        ends.append(at)
    both = jnp.concatenate(arrays, axis=along)
    return tuple(
        jnp.split(
            lax.all_to_all(both, axis, split_axis=split_dim, concat_axis=concat_dim, tiled=True),
            ends,
            axis=along,
        )
    )


def rotate(values, positions):
    half = values.shape[-1] // 2
    freq = THETA ** (-(jnp.arange(half, dtype=jnp.float32) * 2.0 / values.shape[-1]))
    angle = positions.astype(jnp.float32)[..., None] * freq
    angle = jnp.concatenate([angle, angle], -1)[:, :, None, :]
    turned = jnp.concatenate([-values[..., half:], values[..., :half]], -1)
    return values * jnp.cos(angle) + turned * jnp.sin(angle)


def on_device(
    hidden,
    norm_gain,
    w_query,
    w_key,
    w_value,
    bias_query,
    bias_key,
    bias_value,
    key_pages,
    value_pages,
    kv_lengths,
    page_table,
):
    shards = (
        w_query.astype(jnp.bfloat16),
        w_key.astype(jnp.bfloat16),
        w_value.astype(jnp.bfloat16),
    )
    whole = lax.all_gather(hidden, TP, axis=2, tiled=True)
    count, steps, width = whole.shape
    wide = whole.astype(jnp.float32)
    power = jnp.mean(wide * wide, axis=2, keepdims=True)
    normed = (
        (wide * lax.rsqrt(power + EPS) * norm_gain)
        .astype(jnp.bfloat16)
        .reshape(count * steps, width)
    )
    local = (
        two_step_exchange(shards[0], (("tp_0", "tp_1"), "tp_2"), (1, 0), 1, 0),
        two_step_exchange(shards[1], (("tp_0", "tp_1"), "tp_2"), (1, 0), 1, 0),
        two_step_exchange(shards[2], (("tp_0", "tp_1"), "tp_2"), (1, 0), 1, 0),
    )
    pieces = side_by_side((local[0], local[1], local[2]), "replica", 0, 1)
    sums = tuple((jnp.dot(normed, piece, preferred_element_type=jnp.float32) for piece in pieces))
    made = [
        (total + bias).astype(jnp.bfloat16).reshape(count, steps, -1)
        for total, bias in zip(sums, (bias_query, bias_key, bias_value))
    ]
    query, key_new, value_new = (
        lax.all_to_all(made[0], TP, split_axis=0, concat_axis=2, tiled=True),
        *side_by_side_2((made[1], made[2]), TP, 0, 2, 1),
    )
    rows = query.shape[0]
    steps = query.shape[1]
    query = query.reshape(rows, steps, HQ, HD)
    key_new = key_new.reshape(rows, steps, KVH, HD)
    value_new = value_new.reshape(rows, steps, KVH, HD)
    positions = kv_lengths[:, None] + jnp.arange(steps, dtype=jnp.int32)[None, :]
    query_rot = rotate(query.astype(jnp.float32), positions).astype(jnp.bfloat16)
    key_rot = rotate(key_new.astype(jnp.float32), positions).astype(jnp.bfloat16)
    group = HQ // KVH
    scale = 1.0 / HD**0.5
    q_heads = query_rot.reshape(rows, steps, KVH, group, HD)
    keys = jnp.take(key_pages, page_table, axis=0)
    vals = jnp.take(value_pages, page_table, axis=0)
    cache = (
        jnp.einsum("rtkgd,rmknd->rtkgmn", q_heads, keys, preferred_element_type=jnp.float32) * scale
    )
    spot = jnp.arange(MOSTP)[:, None] * PAGE + jnp.arange(PAGE)[None, :]
    live = (spot[None] < kv_lengths[:, None, None])[:, None, None, None]
    cache = jnp.where(live, cache, -1e30)
    causal = jnp.arange(steps)[None, :] <= jnp.arange(steps)[:, None]
    fresh = (
        jnp.einsum("rtkgd,rskd->rtkgs", q_heads, key_rot, preferred_element_type=jnp.float32)
        * scale
    )
    fresh = jnp.where(causal[None, :, None, None, :], fresh, -1e30)
    top = jnp.maximum(jnp.max(cache, axis=(4, 5)), jnp.max(fresh, axis=4))
    e_cache = jnp.where(live, jnp.exp(cache - top[..., None, None]), 0.0)
    e_fresh = jnp.where(causal[None, :, None, None, :], jnp.exp(fresh - top[..., None]), 0.0)
    total = jnp.sum(e_cache, axis=(4, 5)) + jnp.sum(e_fresh, axis=4)
    w_cache = (e_cache / total[..., None, None]).astype(jnp.bfloat16)
    w_fresh = (e_fresh / total[..., None]).astype(jnp.bfloat16)
    out = jnp.einsum("rtkgmn,rmknd->rtkgd", w_cache, vals, preferred_element_type=jnp.float32)
    out = out + jnp.einsum(
        "rtkgs,rskd->rtkgd", w_fresh, value_new, preferred_element_type=jnp.float32
    )
    return out.reshape(rows, steps, HQ * HD).astype(jnp.bfloat16)


def solution(mesh):
    split = Mesh(
        mesh.devices.reshape(mesh.shape["replica"], 4, 2, 2), ("replica", "tp_0", "tp_1", "tp_2")
    )
    in_specs = (
        P("replica", None, TP),
        P(),
        P(REPLICA_TP, None),
        P(REPLICA_TP, None),
        P(REPLICA_TP, None),
        P(TP),
        P(TP),
        P(TP),
        P(REPLICA_TP, None, None, None),
        P(REPLICA_TP, None, None, None),
        P(REPLICA_TP),
        P(REPLICA_TP, None),
    )
    out_specs = P(REPLICA_TP, None, None)
    return jax.shard_map(
        on_device, mesh=split, in_specs=in_specs, out_specs=out_specs, check_vma=False
    )
```

profile of v0, /device:TPU:1, one launch (start us, length us, event | category | flops | bytes accessed | tf_op | source)
XLA Modules:
  0.0 230.4 jit_solution(721957972960235801)
XLA Ops:
  8.9 10.1 %all-to-all-start.4 = ((bf16[2,2,2048]{2,1,0:T(2,128)(2,1)}), bf16[2,2,2048]{2,1,0:T(2,128)(2,1)S(1)}, u32[]{:S(2)}, u32[]{:S(2)}) async-start(bf16[2,2,2048]{2,1,0:T(2,128)(2,1)} %reshape.229), calls=%async_computation.4 | async-start | bytes 32768 | tf_op jit(solution)/shard_map/all_to_all | solution.py:35
  20.6 3.2 %all-to-all-start.2 = ((bf16[2,2,2048]{2,1,0:T(2,128)(2,1)}), bf16[2,2,2048]{2,1,0:T(2,128)(2,1)S(1)}, u32[]{:S(2)}, u32[]{:S(2)}) async-start(bf16[2,2,2048]{2,1,0:T(2,128)(2,1)} %reshape.233), calls=%async_computation.2 | async-start | bytes 32768 | tf_op jit(solution)/shard_map/all_to_all | solution.py:35
  24.7 1.0 convert_element_type.82
  25.7 3.5 %all_to_all.57 = bf16[8,2,16,256]{3,2,0,1:T(8,128)(2,1)S(1)} all-to-all(bf16[8,2,16,256]{3,2,0,1:T(8,128)(2,1)S(1)} %copy.160), channel_id=1, replica_groups=mesh['replica'=32,'tp_0'=4,'tp_1'=2,'tp_2'=2] {'tp_2'}, dimensions={1} | all-to-all | bytes 262144 | tf_op jit(solution)/shard_map/all_to_all | solution.py:35
  29.2 3.3 %all-to-all-start.5 = ((bf16[8,2,512]{2,1,0:T(2,128)(2,1)}), bf16[8,2,512]{2,1,0:T(2,128)(2,1)S(1)}, u32[]{:S(2)}, u32[]{:S(2)}) async-start(bf16[8,2,512]{2,1,0:T(2,128)(2,1)} %reshape.231), calls=%async_computation.5 | async-start | bytes 32768 | tf_op jit(solution)/shard_map/all_to_all | solution.py:35
  33.4 4.3 %all-to-all-done.5 = bf16[8,2,512]{2,1,0:T(2,128)(2,1)S(1)} async-done(((bf16[8,2,512]{2,1,0:T(2,128)(2,1)}), bf16[8,2,512]{2,1,0:T(2,128)(2,1)S(1)}, u32[]{:S(2)}, u32[]{:S(2)}) %all-to-all-start.5) | async-done | bytes 16416 | tf_op jit(solution)/shard_map/all_to_all | solution.py:35
  37.7 3.3 %all-to-all-start.3 = ((bf16[8,2,512]{2,1,0:T(2,128)(2,1)}), bf16[8,2,512]{2,1,0:T(2,128)(2,1)S(1)}, u32[]{:S(2)}, u32[]{:S(2)}) async-start(bf16[8,2,512]{2,1,0:T(2,128)(2,1)} %reshape.235), calls=%async_computation.3 | async-start | bytes 32768 | tf_op jit(solution)/shard_map/all_to_all | solution.py:35
  41.7 4.4 %all-to-all-done.3 = bf16[8,2,512]{2,1,0:T(2,128)(2,1)S(1)} async-done(((bf16[8,2,512]{2,1,0:T(2,128)(2,1)}), bf16[8,2,512]{2,1,0:T(2,128)(2,1)S(1)}, u32[]{:S(2)}, u32[]{:S(2)}) %all-to-all-start.3) | async-done | bytes 16416 | tf_op jit(solution)/shard_map/all_to_all | solution.py:35
  46.1 3.4 %all-to-all-start.1 = ((bf16[8,2,16,256]{3,2,1,0:T(8,128)(2,1)}), bf16[8,2,16,256]{3,2,1,0:T(8,128)(2,1)S(1)}, u32[]{:S(2)}, u32[]{:S(2)}) async-start(bf16[8,2,16,256]{3,2,1,0:T(8,128)(2,1)} %copy.161), calls=%async_computation.1 | async-start | bytes 262144 | tf_op jit(solution)/shard_map/all_to_all | solution.py:35
  49.7 5.4 %all-to-all-done.1 = bf16[8,2,16,256]{3,2,1,0:T(8,128)(2,1)S(1)} async-done(((bf16[8,2,16,256]{3,2,1,0:T(8,128)(2,1)}), bf16[8,2,16,256]{3,2,1,0:T(8,128)(2,1)S(1)}, u32[]{:S(2)}, u32[]{:S(2)}) %all-to-all-start.1) | async-done | bytes 131104 | tf_op jit(solution)/shard_map/all_to_all | solution.py:35
  56.1 2.7 %gather_fusion.1 = bf16[24,4,128,128]{3,2,1,0:T(8,128)(2,1)} fusion(bf16[16,4,128,128]{3,2,1,0:T(8,128)(2,1)S(1)} %copy-done, s32[1024]{0:T(1024)S(1)} %pad_clamp_fusion), kind=kCustom, calls=%fused_computation.1.clone | custom fusion | bytes 6291552 | tf_op jit(solution)/shard_map/jit(_take)/gather | solution.py:130
  58.8 4.3 %gather_fusion = bf16[24,4,128,128]{3,2,1,0:T(8,128)(2,1)} fusion(bf16[16,4,128,128]{3,2,1,0:T(8,128)(2,1)} %param.23, s32[1024]{0:T(1024)S(1)} %pad_clamp_fusion), kind=kCustom, calls=%fused_computation.clone | custom fusion | bytes 6291552 | tf_op jit(solution)/shard_map/jit(_take)/gather | solution.py:131
  63.6 3.8 %fusion = f32[48,4]{1,0:T(8,128)S(1)} fusion(bf16[48,4,8192]{2,1,0:T(4,128)(2,1)} %all-gather.3.cloned.1.call-done), kind=kLoop, calls=%fused_computation.4 | loop fusion | flops 4718400 | bytes 3146496 | tf_op jit(solution)/shard_map/reduce_sum | solution.py:98
  67.4 3.6 %fusion.2 = bf16[48,4,8192]{2,1,0:T(4,128)(2,1)} fusion(bf16[48,4,8192]{2,1,0:T(4,128)(2,1)S(1)} %copy-done.1, f32[8192]{0:T(1024)S(1)} %copy-done.3, f32[48,4]{1,0:T(8,128)S(1)} %add_rsqrt_fusion), kind=kLoop, calls=%fused_computation.6 | loop fusion | flops 6291456 | bytes 6324992 | tf_op jit(solution)/shard_map/convert_element_type | solution.py:101
  71.0 5.5 %reshape.179 = bf16[192,8192]{1,0:T(8,128)(2,1)} reshape(bf16[48,4,8192]{2,1,0:T(4,128)(2,1)} %fusion.2) | data formatting | bytes 6291456 | tf_op jit(solution)/shard_map/reshape | solution.py:102
  76.5 106.5 %all-gather.5.cloned.1.call-done = bf16[8192,320]{1,0:T(8,128)(2,1)} async-done(((bf16[256,320]{1,0:T(8,128)(2,1)}), bf16[8192,320]{1,0:T(8,128)(2,1)}) %all-gather.5.cloned.1.call-update) | async-done | bytes 5242896 | tf_op jit(solution)/shard_map/all_gather | solution.py:48
  183.0 3.7 %fusion.44 = bf16[192,32]{0,1:T(8,128)(2,1)S(1)} fusion(bf16[192,8192]{1,0:T(8,128)(2,1)} %reshape.179, bf16[8192,320]{1,0:T(8,128)(2,1)} %all-gather.5.cloned.1.call-done, f32[32]{0:T(128)S(1)} %copy-done.6), kind=kOutput, calls=%fused_computation.42 | convolution fusion | flops 100675584 | bytes 5255296 | tf_op jit(solution)/shard_map/dot_general | solution.py:110
  186.8 4.5 %fusion.41 = bf16[192,32]{0,1:T(8,128)(2,1)S(1)} fusion(bf16[192,8192]{1,0:T(8,128)(2,1)} %reshape.179, bf16[8192,320]{1,0:T(8,128)(2,1)} %all-gather.5.cloned.1.call-done, f32[32]{0:T(128)S(1)} %copy-done.7), kind=kOutput, calls=%fused_computation.41 | convolution fusion | flops 100675584 | bytes 5255296 | tf_op jit(solution)/shard_map/dot_general | solution.py:110
  192.3 8.0 %all-to-all-start.7 = ((bf16[16,2,384]{2,1,0:T(2,128)(2,1)}), bf16[16,2,384]{2,1,0:T(2,128)(2,1)S(1)}, u32[]{:S(2)}, u32[]{:S(2)}) async-start(bf16[16,2,384]{2,1,0:T(2,128)(2,1)} %reshape.237), calls=%async_computation.7 | async-start | bytes 49152 | tf_op jit(solution)/shard_map/all_to_all | solution.py:60
  200.2 4.1 %fusion.28 = bf16[192,256]{1,0:T(8,128)(2,1)S(1)} fusion(bf16[192,8192]{1,0:T(8,128)(2,1)} %reshape.179, bf16[8192,320]{1,0:T(8,128)(2,1)} %all-gather.5.cloned.1.call-done, f32[256]{0:T(256)S(1)} %copy-done.8), kind=kOutput, calls=%fused_computation.33 | convolution fusion | flops 805404672 | bytes 7439360 | tf_op jit(solution)/shard_map/dot_general | solution.py:110
  205.9 4.9 %all-to-all-start.6 = ((bf16[48,4,256]{2,1,0:T(4,128)(2,1)}), bf16[48,4,256]{2,1,0:T(4,128)(2,1)S(1)}, u32[]{:S(2)}, u32[]{:S(2)}) async-start(bf16[48,4,256]{2,1,0:T(4,128)(2,1)} %reshape.186), calls=%async_computation.6 | async-start | bytes 196608 | tf_op jit(solution)/shard_map/all_to_all | solution.py:116
  211.2 5.5 %all-to-all-done.6 = bf16[48,4,256]{2,1,0:T(4,128)(2,1)S(1)} async-done(((bf16[48,4,256]{2,1,0:T(4,128)(2,1)}), bf16[48,4,256]{2,1,0:T(4,128)(2,1)S(1)}, u32[]{:S(2)}, u32[]{:S(2)}) %all-to-all-start.6) | async-done | bytes 98336 | tf_op jit(solution)/shard_map/all_to_all | solution.py:116
  217.6 3.4 %bitcast_reduce_fusion = (f32[3,4,4,8]{3,1,2,0:T(4,128)S(1)}, f32[3,4,8,128,4,8]{3,5,4,2,1,0:T(8,128)S(1)}) fusion(bf16[3,8,4,128,128]{4,3,2,1,0:T(8,128)(2,1)} %bitcast.120, pred[3,8]{1,0:T(4,128)(4,1)S(1)} %compare_and_fusion, pred[3,8,128]{2,1,0:T(8,128)(4,1)S(1)} %broadcast_compare_fusion, bf16[3,4,4,8,128]{4,3,2,1,0:T(8,128)(2,1)S(1)} %fusion.53), kind=kOutput, calls=%fused_computation.22 | convolution fusion | flops 103415424 | bytes 4821528 | tf_op jit(solution)/shard_map/rtkgd,rmknd->rtkgmn/dot_general | solution.py:133
  221.6 1.0 fusion.22
  (84 shorter events, 13.4 us)
Async XLA Ops:
  6.5 49.5 %copy-start = (bf16[16,4,128,128]{3,2,1,0:T(8,128)(2,1)S(1)}, bf16[16,4,128,128]{3,2,1,0:T(8,128)(2,1)}, u32[]{:S(2)}) copy-start(bf16[16,4,128,128]{3,2,1,0:T(8,128)(2,1)} %param.22) | copy-start | bytes 6291460
  6.5 49.4 %copy-start.4 = (s32[3,8]{1,0:T(4,128)S(1)}, s32[3,8]{1,0:T(4,128)}, u32[]{:S(2)}) copy-start(s32[3,8]{1,0:T(4,128)} %param.25) | copy-start | bytes 292
  6.5 57.0 %all-gather.3.cloned.1.call-start = ((), (), s32[]{:S(2)}) async-start(), calls=%async_computation.8 | async-start | bytes 3342336 | tf_op jit(solution)/shard_map/all_gather | solution.py:95
  8.9 11.7 %all-to-all-start.4 = ((bf16[2,2,2048]{2,1,0:T(2,128)(2,1)}), bf16[2,2,2048]{2,1,0:T(2,128)(2,1)S(1)}, u32[]{:S(2)}, u32[]{:S(2)}) async-start(bf16[2,2,2048]{2,1,0:T(2,128)(2,1)} %reshape.229), calls=%async_computation.4 | async-start | bytes 32768 | tf_op jit(solution)/shard_map/all_to_all | solution.py:35
  20.6 5.2 %all-to-all-start.2 = ((bf16[2,2,2048]{2,1,0:T(2,128)(2,1)}), bf16[2,2,2048]{2,1,0:T(2,128)(2,1)S(1)}, u32[]{:S(2)}, u32[]{:S(2)}) async-start(bf16[2,2,2048]{2,1,0:T(2,128)(2,1)} %reshape.233), calls=%async_computation.2 | async-start | bytes 32768 | tf_op jit(solution)/shard_map/all_to_all | solution.py:35
  29.2 8.4 %all-to-all-start.5 = ((bf16[8,2,512]{2,1,0:T(2,128)(2,1)}), bf16[8,2,512]{2,1,0:T(2,128)(2,1)S(1)}, u32[]{:S(2)}, u32[]{:S(2)}) async-start(bf16[8,2,512]{2,1,0:T(2,128)(2,1)} %reshape.231), calls=%async_computation.5 | async-start | bytes 32768 | tf_op jit(solution)/shard_map/all_to_all | solution.py:35
  37.7 8.4 %all-to-all-start.3 = ((bf16[8,2,512]{2,1,0:T(2,128)(2,1)}), bf16[8,2,512]{2,1,0:T(2,128)(2,1)S(1)}, u32[]{:S(2)}, u32[]{:S(2)}) async-start(bf16[8,2,512]{2,1,0:T(2,128)(2,1)} %reshape.235), calls=%async_computation.3 | async-start | bytes 32768 | tf_op jit(solution)/shard_map/all_to_all | solution.py:35
  46.1 9.0 %all-to-all-start.1 = ((bf16[8,2,16,256]{3,2,1,0:T(8,128)(2,1)}), bf16[8,2,16,256]{3,2,1,0:T(8,128)(2,1)S(1)}, u32[]{:S(2)}, u32[]{:S(2)}) async-start(bf16[8,2,16,256]{3,2,1,0:T(8,128)(2,1)} %copy.161), calls=%async_computation.1 | async-start | bytes 262144 | tf_op jit(solution)/shard_map/all_to_all | solution.py:35
  49.5 133.5 %all-gather.5.cloned.1.call-start = ((), (), s32[]{:S(2)}) async-start(), calls=%async_computation.9 | async-start | bytes 6488064 | tf_op jit(solution)/shard_map/all_gather | solution.py:48
  58.8 4.4 %copy-start.5 = (s32[3]{0:T(128)S(1)}, s32[3]{0:T(128)}, u32[]{:S(2)}) copy-start(s32[3]{0:T(128)} %param.24) | copy-start | bytes 40
  63.1 4.3 %copy-start.3 = (f32[8192]{0:T(1024)S(1)}, f32[8192]{0:T(1024)}, u32[]{:S(2)}) copy-start(f32[8192]{0:T(1024)} %param.15) | copy-start | bytes 98308
  63.6 3.8 %copy-start.1 = (bf16[48,4,8192]{2,1,0:T(4,128)(2,1)S(1)}, bf16[48,4,8192]{2,1,0:T(4,128)(2,1)}, u32[]{:S(2)}) copy-start(bf16[48,4,8192]{2,1,0:T(4,128)(2,1)} %all-gather.3.cloned.1.call-done) | copy-start | bytes 9437188
  71.0 112.0 %copy-start.6 = (f32[32]{0:T(128)S(1)}, f32[32]{0:T(128)}, u32[]{:S(2)}) copy-start(f32[32]{0:T(128)} %param.20) | copy-start | bytes 388
  76.5 110.3 %copy-start.7 = (f32[32]{0:T(128)S(1)}, f32[32]{0:T(128)}, u32[]{:S(2)}) copy-start(f32[32]{0:T(128)} %param.21) | copy-start | bytes 388
  186.7 13.5 %copy-start.8 = (f32[256]{0:T(256)S(1)}, f32[256]{0:T(256)}, u32[]{:S(2)}) copy-start(f32[256]{0:T(256)} %param.19) | copy-start | bytes 3076
  192.3 13.6 %all-to-all-start.7 = ((bf16[16,2,384]{2,1,0:T(2,128)(2,1)}), bf16[16,2,384]{2,1,0:T(2,128)(2,1)S(1)}, u32[]{:S(2)}, u32[]{:S(2)}) async-start(bf16[16,2,384]{2,1,0:T(2,128)(2,1)} %reshape.237), calls=%async_computation.7 | async-start | bytes 49152 | tf_op jit(solution)/shard_map/all_to_all | solution.py:60
  205.9 10.7 %all-to-all-start.6 = ((bf16[48,4,256]{2,1,0:T(4,128)(2,1)}), bf16[48,4,256]{2,1,0:T(4,128)(2,1)S(1)}, u32[]{:S(2)}, u32[]{:S(2)}) async-start(bf16[48,4,256]{2,1,0:T(4,128)(2,1)} %reshape.186), calls=%async_computation.6 | async-start | bytes 196608 | tf_op jit(solution)/shard_map/all_to_all | solution.py:116
  217.6 4.0 %copy-start.2 = (bf16[24,4,128,128]{3,2,1,0:T(8,128)(2,1)S(1)}, bf16[24,4,128,128]{3,2,1,0:T(8,128)(2,1)}, u32[]{:S(2)}) copy-start(bf16[24,4,128,128]{3,2,1,0:T(8,128)(2,1)} %gather_fusion) | copy-start | bytes 9437188
Sparse Core Ops, SparseCore 0:
  9.4 53.6 all-gather.2
  66.2 116.7 all-gather.4
where the time goes:
time: 231 us; the launch traced here: 230 us
  waiting for transfers between devices  128 us (55%)
  starting transfers between devices  36.2 us (16%)
  local copies, waits for them, and re-layouts  19.6 us (8%)
  matrix products  17.6 us (8%)
  between operations  13.8 us (6%)
  other arithmetic  12.1 us (5%)
  blocking collectives  3.51 us (2%)
    all_gather x1, waiting for transfers between devices, side_by_side(): out = lax.all_gather(both, axis, axis=dim, tiled=True)  106 us
    all_to_all x5, starting transfers between devices, exchange_in_order(): out = lax.all_to_all(out, axes[k], k, k, tiled=True)  23.3 us
    all_to_all x5, waiting for transfers between devices, exchange_in_order(): out = lax.all_to_all(out, axes[k], k, k, tiled=True)  14.1 us
    dot_general x3, matrix products, on_device(): jnp.dot(normed, piece, preferred_element_type=jnp.float32)  12.4 us
    all_to_all x1, starting transfers between devices, side_by_side_2(): lax.all_to_all(both, axis, split_axis=split_dim, concat_axis=concat_dim,...  7.95 us
    reshape x1, local copies, waits for them, and re-layouts, on_device(): normed = (wide * lax.rsqrt(power + EPS) * norm_gain).astype(jnp.bfloat16)...  5.51 us
    all_to_all x1, waiting for transfers between devices, on_device(): lax.all_to_all(made[0], TP, split_axis=0, concat_axis=2, tiled=True)  5.47 us
    all_to_all x1, starting transfers between devices, on_device(): lax.all_to_all(made[0], TP, split_axis=0, concat_axis=2, tiled=True)  4.89 us
  transfers between devices with their start and end apart: 9, of which 6 were waited for; matrix products, arithmetic and copies ran while one was open for 14% of the time, Pallas kernels for 0%

commit v1 on v0

v1 whole, which is shorter than its diff:
```python
import functools

import jax
import jax.numpy as jnp
from jax import lax
from jax.experimental import pallas as pl
from jax.experimental.pallas import tpu as pltpu
from jax.sharding import Mesh
from jax.sharding import PartitionSpec as P

HD = 128
HQ = 32
KVH = 4
GROUP = HQ // KVH
PAGE = 128
MOSTP = 8
STEPS = 4
ROWS = 3
OWN = ROWS * STEPS
D = 8192
EPS = 1e-06
THETA = 1000000.0
MESH = pl.DeviceIdType.MESH
AXES = ("yh", "z", "x", "yl", "c")
TP = ("x", "yl", "c")
REPLICA = ("yh", "z")
COLS = 640
KB = 512
BR = 192
RT = 96


def remote(src, dst, send, recv, where):
    return pltpu.make_async_remote_copy(
        src_ref=src, dst_ref=dst, send_sem=send, recv_sem=recv, device_id=where, device_id_type=MESH
    )


def project_kernel(
    x_ref, w_ref, st_ref,
    out_ref, sto_ref,
    xg, a1, wz, acc, dsend, drecv, rsend, rrecv, fin, ysend, yrecv, strecv,
    xs, xr, a1s, a1r, a2s, a2r, ws, wr, sts, strs, d2s, d2r, rss, rrs, yss, yrs,
):
    yh, z, x, yl, c = (lax.axis_index(a) for a in AXES)
    y = yh * 2 + yl
    tp = x * 4 + yl * 2 + c
    zb = lax.rem(z // 2, 2)

    def at_y(k):
        return {"yh": k // 2, "yl": lax.rem(k, 2)}

    def at_tp(k):
        return {"x": k // 4, "yl": lax.rem(k // 2, 2), "c": lax.rem(k, 2)}

    def add(a, k, n):
        return lax.rem(a + (k + n) % n, n)

    barrier = pltpu.get_barrier_semaphore()
    for d in range(1, 16):
        pl.semaphore_signal(barrier, inc=1, device_id=at_tp(add(tp, d, 16)), device_id_type=MESH)
    for d in range(1, 4):
        for k in range(2):
            pl.semaphore_signal(
                barrier, inc=1, device_id={"yh": add(yh, d, 4), "yl": k}, device_id_type=MESH
            )
    for d in (1, -1):
        pl.semaphore_signal(barrier, inc=1, device_id={"z": add(z, d, 8)}, device_id_type=MESH)
    pl.semaphore_wait(barrier, 23)

    y_next = (at_y(add(y, 1, 8)), at_y(add(y, -1, 8)))
    z_next = ({"z": add(z, 1, 8)}, {"z": add(z, -1, 8)})

    def x_copy(s, h, way):
        o = add(y, -(s - 1) if way == 0 else s - 1, 8)
        rows = pl.ds(RT * h, RT)
        src = x_ref.at[rows] if s == 1 else xg.at[o, rows]
        return remote(
            src, xg.at[o, rows], xs.at[way, s - 1, h], xr.at[way, s - 1, h], y_next[way]
        )

    def x_wait(s, h, way):
        o = add(y, -s if way == 0 else s, 8)
        dst = xg.at[o, pl.ds(RT * h, RT)]
        remote(dst, dst, xs.at[way, s - 1, h], xr.at[way, s - 1, h], y_next[way]).wait_recv()

    def goes(s, h, way):
        return s <= 3 or (s == 4 and h == way)

    def origin_w(s, way):
        o = add(z, -s if way == 0 else s, 8)
        return o, lax.rem(o // 2, 2) == c, (o // 4) * 2 + lax.rem(o, 2)

    def w_copy(s, h, way):
        _, mine, j = origin_w(s - 1, way)
        part = wz.at[j, pl.ds(2 * h, 2)]
        return mine, remote(
            part, part, ws.at[way, s - 1, h], wr.at[way, s - 1, h], z_next[way]
        )

    def w_send(s, h, way):
        mine, copy = w_copy(s, h, way)

        @pl.when(mine)
        def _():
            copy.start()

    def w_step(s, h, way):
        _, mine, j = origin_w(s, way)
        part = wz.at[j, pl.ds(2 * h, 2)]

        @pl.when(mine)
        def _():
            remote(
                part, part, ws.at[way, s - 1, h], wr.at[way, s - 1, h], z_next[way]
            ).wait_recv()
            if goes(s + 1, h, way):
                w_copy(s + 1, h, way)[1].start()

    def x_step(s, h):
        for way in range(2):
            if goes(s, h, way):
                x_wait(s, h, way)
                if goes(s + 1, h, way):
                    x_copy(s + 1, h, way).start()

    def a1_copy(d):
        k = add(y, d, 8)
        return remote(w_ref.at[k], a1.at[y], a1s.at[d], a1r.at[y], at_y(k))

    for d in (4, 3, 5, 2, 6, 1, 7):
        a1_copy(d).start()
    for h in range(2):
        for way in range(2):
            x_copy(1, h, way).start()

    def st_copy(d):
        k = add(tp, d, 16)
        return remote(st_ref.at[k], strecv.at[tp], sts.at[d], strs.at[tp], at_tp(k))

    for d in range(1, 16):
        st_copy(d).start()
    a1[y] = w_ref[y]
    xg[y] = x_ref[...]
    strecv[tp] = st_ref[tp]

    for d in range(1, 8):
        k = add(y, d, 8)
        remote(a1.at[k], a1.at[k], a1s.at[d], a1r.at[k], at_y(k)).wait_recv()

    own_j = (z // 4) * 2 + lax.rem(z, 2)

    def a2_copy(d):
        k = add(x, d, 4)
        return remote(
            a1.at[pl.ds(2 * k, 2)],
            wz.at[own_j, x, :, c],
            a2s.at[d],
            a2r.at[x * 2 + c],
            {"x": k, "c": zb},
        )

    for d in (2, 1, 3):
        a2_copy(d).start()

    @pl.when(zb != c)
    def _():
        a2_copy(0).start()

    @pl.when(zb == c)
    def _():
        wz[own_j, x, :, c] = a1[pl.ds(2 * x, 2)]

    x_step(1, 0)
    x_step(1, 1)

    @pl.when(zb == c)
    def _():
        for d in range(8):
            k = add(x * 2 + c, d, 8)
            kx, kc = k // 2, lax.rem(k, 2)
            dst = wz.at[own_j, kx, :, kc]
            if d > 0:
                remote(dst, dst, a2s.at[0], a2r.at[k], {"x": kx, "c": kc}).wait_recv()

    for h in range(2):
        for way in range(2):
            w_send(1, h, way)
    x_step(2, 0)
    x_step(2, 1)
    for s in range(1, 5):
        for h in range(2):
            for way in range(2):
                if goes(s, h, way):
                    w_step(s, h, way)
        if s == 1:
            x_step(3, 0)
            x_step(3, 1)
        if s == 2:
            x_step(4, 0)
            x_step(4, 1)

    def one_block(b, carry):
        total = jnp.zeros((BR, COLS), jnp.float32)
        for k in range(2):
            total += jnp.dot(
                xg[b * 2 + k],
                wz[2 * k : 2 * k + 2].reshape(KB, COLS),
                preferred_element_type=jnp.float32,
            )
        acc[b] = total
        return carry

    lax.fori_loop(0, 4, one_block, 0)

    def rows_for(kx, kc):
        at = pl.multiple_of((kx * 2 + kc) * 24, 8)
        return acc[:, pl.ds(at, 24), :].reshape(RT, COLS)

    oc = 1 - c
    order = (2, 1, 3, 0)

    def d_copy(d):
        return remote(dsend.at[d], drecv.at[d], d2s.at[d], d2r.at[d], {"c": oc})

    for d in order:
        dsend[d] = rows_for(add(x, d, 4), oc).astype(jnp.bfloat16)
        d_copy(d).start()

    def r_copy(d):
        k = add(x, d, 4)
        return remote(rsend.at[d], rrecv.at[x], rss.at[d], rrs.at[x], {"x": k})

    for d in order:
        d_copy(d).wait_recv()
        total = rows_for(add(x, d, 4), c) + drecv[d].astype(jnp.float32)
        if d:
            rsend[d] = total.astype(jnp.bfloat16)
            r_copy(d).start()
        else:
            fin[pl.ds(0, RT), :] = total
    fin[pl.ds(RT, 8), :] = jnp.zeros((8, COLS), jnp.float32)
    for d in (1, 3, 2):
        k = add(x, d, 4)
        remote(rrecv.at[k], rrecv.at[k], rss.at[d], rrs.at[k], {"x": k}).wait_recv()
        fin[pl.ds(0, RT), :] += rrecv[k].astype(jnp.float32)

    def y_copy(d):
        k = add(y, d, 8)
        return remote(ysend.at[k], yrecv.at[y], yss.at[d], yrs.at[y], at_y(k))

    for k in range(8):
        ysend[k] = fin[pl.ds(OWN * k, 16), :].astype(jnp.bfloat16)
    for d in (4, 3, 5, 2, 6, 1, 7):
        y_copy(d).start()
    out_ref[y] = ysend[y]
    for d in range(1, 16):
        k = add(tp, d, 16)
        remote(strecv.at[k], strecv.at[k], sts.at[d], strs.at[k], at_tp(k)).wait_recv()
    sto_ref[...] = strecv[...]
    for d in range(1, 8):
        k = add(y, d, 8)
        remote(yrecv.at[k], yrecv.at[k], yss.at[d], yrs.at[k], at_y(k)).wait_recv()
        out_ref[k] = yrecv[k]

    for d in range(1, 8):
        a1_copy(d).wait_send()
        y_copy(d).wait_send()
    for d in range(1, 16):
        st_copy(d).wait_send()
    for d in range(1, 4):
        a2_copy(d).wait_send()
        r_copy(d).wait_send()

    @pl.when(zb != c)
    def _():
        a2_copy(0).wait_send()

    for d in range(4):
        d_copy(d).wait_send()
    for s in range(1, 5):
        for h in range(2):
            for way in range(2):
                if goes(s, h, way):
                    x_copy(s, h, way).wait_send()
                    mine, copy = w_copy(s, h, way)

                    @pl.when(mine)
                    def _(copy=copy):
                        copy.wait_send()


def project(x, w, st):
    vm = pltpu.VMEM
    dma = pltpu.SemaphoreType.DMA
    bf = jnp.bfloat16
    return pl.pallas_call(
        project_kernel,
        out_shape=(
            jax.ShapeDtypeStruct((8, 16, COLS), bf),
            jax.ShapeDtypeStruct((16, 8, 128), jnp.float32),
        ),
        in_specs=[pl.BlockSpec(memory_space=vm)] * 3,
        out_specs=(pl.BlockSpec(memory_space=vm),) * 2,
        scratch_shapes=[
            vm((8, BR, KB), bf),
            vm((8, 16, COLS), bf),
            vm((4, 4, 2, 2, 16, COLS), bf),
            vm((4, BR, COLS), jnp.float32),
            vm((4, RT, COLS), bf),
            vm((4, RT, COLS), bf),
            vm((4, RT, COLS), bf),
            vm((4, RT, COLS), bf),
            vm((RT + 8, COLS), jnp.float32),
            vm((8, 16, COLS), bf),
            vm((8, 16, COLS), bf),
            vm((16, 8, 128), jnp.float32),
            dma((2, 4, 2)), dma((2, 4, 2)),
            dma((8,)), dma((8,)),
            dma((4,)), dma((8,)),
            dma((2, 4, 2)), dma((2, 4, 2)),
            dma((16,)), dma((16,)),
            dma((4,)), dma((4,)),
            dma((4,)), dma((4,)),
            dma((8,)), dma((8,)),
        ],
        compiler_params=pltpu.CompilerParams(collective_id=0, has_side_effects=True),
        name="project",
    )(x, w, st)


def attend_kernel(len_ref, table_ref, qkv_ref, st_ref, kp_ref, vp_ref, out_ref, kbuf, vbuf, ksem, vsem):
    def page(r, m):
        at = table_ref[r, m]
        return (
            pltpu.make_async_copy(kp_ref.at[at], kbuf.at[r, :, m], ksem.at[r, m]),
            pltpu.make_async_copy(vp_ref.at[at], vbuf.at[r, :, m], vsem.at[r, m]),
        )

    for r in range(ROWS):
        for m in range(MOSTP):
            for copy in page(r, m):
                copy.start()

    rows16 = lax.broadcasted_iota(jnp.int32, (16, 128), 0)
    lanes16 = lax.broadcasted_iota(jnp.int32, (16, 128), 1)
    squares = jnp.sum(st_ref[:, 4, :], axis=0, keepdims=True)
    power = jnp.sum(
        jnp.where(rows16 == lanes16, jnp.broadcast_to(squares, (16, 128)), 0.0),
        axis=1,
        keepdims=True,
    )
    inv = lax.rsqrt(power * (1.0 / D) + EPS)
    keep = rows16 < OWN
    low = lanes16 < HD // 2

    row_of = rows16 // STEPS
    length = jnp.where(row_of == 0, len_ref[0], jnp.where(row_of == 1, len_ref[1], len_ref[2]))
    position = (length + lax.rem(rows16, STEPS)).astype(jnp.float32)
    pair = lax.rem(lanes16, HD // 2).astype(jnp.float32)
    freq = jnp.power(THETA, -(pair * 2.0 / HD))
    angle = position * freq
    cos, sin = jnp.cos(angle), jnp.sin(angle)
    sin = jnp.where(low, -sin, sin)

    def made(total, bias):
        value = (total * inv + bias).astype(jnp.bfloat16).astype(jnp.float32)
        return jnp.where(keep, value, 0.0)

    def rotated(value):
        return (value * cos + pltpu.roll(value, HD // 2, 1) * sin).astype(jnp.bfloat16)

    sel_row = lax.broadcasted_iota(jnp.int32, (32, 128), 0)
    sel_col = lax.broadcasted_iota(jnp.int32, (32, 128), 1)
    new_row = lax.broadcasted_iota(jnp.int32, (32, 16), 0)
    new_col = lax.broadcasted_iota(jnp.int32, (32, 16), 1)
    spot = lax.broadcasted_iota(jnp.int32, (32, MOSTP * PAGE), 1)
    scale = 1.0 / HD**0.5

    q_all, k_all, v_all = [], [], []
    for kh in range(KVH):
        heads = []
        for g in range(GROUP):
            h = kh * GROUP + g
            total = qkv_ref[h // 4, :, (h % 4) * HD : (h % 4 + 1) * HD].astype(jnp.float32)
            heads.append(rotated(made(total, st_ref[h // 2, h % 2 : h % 2 + 1, :])))
        q_all.append(jnp.concatenate(heads, axis=0))
        t0 = qkv_ref[2 * kh, :, 4 * HD : 5 * HD].astype(jnp.float32)
        t1 = qkv_ref[2 * kh + 1, :, 4 * HD : 5 * HD].astype(jnp.float32)
        k_bias = sum(st_ref[4 * kh + i, 2:3, :] for i in range(4))
        v_bias = sum(st_ref[4 * kh + i, 3:4, :] for i in range(4))
        k_sum = jnp.where(low, t0, pltpu.roll(t1, HD // 2, 1))
        v_sum = jnp.where(low, pltpu.roll(t0, HD // 2, 1), t1)
        k_all.append(rotated(made(k_sum, k_bias)))
        v_all.append(made(v_sum, v_bias).astype(jnp.bfloat16))

    contract = (((1,), (1,)), ((), ()))
    for r in range(ROWS):
        for m in range(MOSTP):
            for copy in page(r, m):
                copy.wait()
        want = (sel_row % GROUP) * 16 + r * STEPS + sel_row // GROUP
        pick = jnp.where(sel_col == want, 1.0, 0.0).astype(jnp.bfloat16)
        live = spot < len_ref[r]
        fresh_live = (new_col // STEPS == r) & (lax.rem(new_col, STEPS) <= new_row // GROUP)
        for kh in range(KVH):
            q = jnp.dot(pick, q_all[kh], preferred_element_type=jnp.float32).astype(jnp.bfloat16)
            keys = kbuf[r, kh].reshape(MOSTP * PAGE, HD)
            vals = vbuf[r, kh].reshape(MOSTP * PAGE, HD)
            cache = lax.dot_general(q, keys, contract, preferred_element_type=jnp.float32) * scale
            cache = jnp.where(live, cache, -1e30)
            fresh = (
                lax.dot_general(q, k_all[kh], contract, preferred_element_type=jnp.float32) * scale
            )
            fresh = jnp.where(fresh_live, fresh, -1e30)
            top = jnp.maximum(
                jnp.max(cache, axis=1, keepdims=True), jnp.max(fresh, axis=1, keepdims=True)
            )
            e_cache = jnp.where(live, jnp.exp(cache - top), 0.0)
            e_fresh = jnp.where(fresh_live, jnp.exp(fresh - top), 0.0)
            total = jnp.sum(e_cache, axis=1, keepdims=True) + jnp.sum(e_fresh, axis=1, keepdims=True)
            share = 1.0 / total
            w_cache = (e_cache * share).astype(jnp.bfloat16)
            w_fresh = (e_fresh * share).astype(jnp.bfloat16)
            out = jnp.dot(w_cache, vals, preferred_element_type=jnp.float32)
            out += jnp.dot(w_fresh, v_all[kh], preferred_element_type=jnp.float32)
            for t in range(STEPS):
                out_ref[r, t, kh * GROUP : (kh + 1) * GROUP, :] = out[t * GROUP : (t + 1) * GROUP, :]


def attend(lengths, table, qkv, st, key_pages, value_pages):
    vm = pltpu.VMEM
    return pl.pallas_call(
        attend_kernel,
        out_shape=jax.ShapeDtypeStruct((ROWS, STEPS, HQ, HD), jnp.float32),
        in_specs=[pl.BlockSpec(memory_space=pltpu.SMEM)] * 2
        + [pl.BlockSpec(memory_space=vm)] * 2
        + [pl.BlockSpec(memory_space=pl.ANY)] * 2,
        out_specs=pl.BlockSpec(memory_space=vm),
        scratch_shapes=[
            vm((ROWS, KVH, MOSTP, PAGE, HD), jnp.bfloat16),
            vm((ROWS, KVH, MOSTP, PAGE, HD), jnp.bfloat16),
            pltpu.SemaphoreType.DMA((ROWS, MOSTP)),
            pltpu.SemaphoreType.DMA((ROWS, MOSTP)),
        ],
        name="attend",
    )(lengths, table, qkv, st, key_pages, value_pages)


def on_device(
    hidden,
    norm_gain,
    w_query,
    w_key,
    w_value,
    bias_query,
    bias_key,
    bias_value,
    key_pages,
    value_pages,
    kv_lengths,
    page_table,
):
    tp = lax.axis_index(TP)
    block = lax.axis_index(REPLICA) * 16 + tp
    gain = lax.dynamic_slice(norm_gain, (block * 16,), (16,))
    weights = jnp.concatenate(
        [w_query.reshape(16, 8, 512), w_key.reshape(16, 8, 64), w_value.reshape(16, 8, 64)], axis=2
    )
    weights = (weights * gain[:, None, None]).astype(jnp.bfloat16).transpose(1, 0, 2)
    rows = hidden.reshape(4, 2, 2, OWN, KB).transpose(0, 2, 1, 3, 4).reshape(BR, KB)
    wide = hidden.astype(jnp.float32)
    squares = jnp.sum(wide * wide, axis=2).reshape(16, 1, OWN)
    lane = jnp.arange(128)
    place = (lane // 32) == lax.rem(tp, 4)
    k_bias = jnp.where(place, jnp.tile(bias_key, 4), 0.0)
    v_bias = jnp.where(place, jnp.tile(bias_value, 4), 0.0)
    shared = jnp.concatenate([bias_query.reshape(2, 128), k_bias[None], v_bias[None]], axis=0)
    stats = jnp.concatenate(
        [
            jnp.broadcast_to(shared[None], (16, 4, 128)),
            jnp.pad(squares, ((0, 0), (0, 3), (0, 128 - OWN))),
        ],
        axis=1,
    )
    stats = jnp.pad(stats, ((0, 0), (0, 8 - stats.shape[1]), (0, 0)))
    qkv, stats = project(rows, weights, stats)
    out = attend(kv_lengths, page_table, qkv, stats, key_pages, value_pages)
    return out.astype(jnp.bfloat16).reshape(ROWS, STEPS, HQ * HD)


def solution(mesh):
    split = Mesh(mesh.devices.reshape(4, 8, 4, 2, 2), AXES)
    both = REPLICA + TP
    in_specs = (
        P(REPLICA, None, TP),
        P(),
        P(both, None),
        P(both, None),
        P(both, None),
        P(TP),
        P(TP),
        P(TP),
        P(both, None, None, None),
        P(both, None, None, None),
        P(both),
        P(both, None),
    )
    return jax.shard_map(
        on_device, mesh=split, in_specs=in_specs, out_specs=P(both, None, None), check_vma=False
    )
```

time: 231 us -> 85 us (0.37)
  waiting for transfers between devices: 128 us -> 0 us
  Pallas kernels: 0 us -> 73.9 us
  starting transfers between devices: 36.2 us -> 0 us
  matrix products: 17.6 us -> 0 us
  between operations: 13.8 us -> 0.05 us
  local copies, waits for them, and re-layouts: 19.6 us -> 6.5 us
  other arithmetic: 12.1 us -> 4.17 us
  blocking collectives: 3.51 us -> 0 us
    all_gather x2 -> x0, waiting for transfers between devices: 106 us -> none  [the longest x1 106 us: side_by_side(): out = lax.all_gather(both, axis, axis=dim, tiled=True)]
    pallas_call x0 -> x2, Pallas kernels: none -> 73.9 us  [the longest x1 63.6 us: project(): pl.pallas_call(project_kernel, out_shape=(jax.ShapeDtypeStruct((8, 16, CO...]
    all_to_all x7 -> x0, starting transfers between devices: 36.2 us -> none  [the longest x5 23.3 us: exchange_in_order(): out = lax.all_to_all(out, axes[k], k, k, tiled=True)]
    all_to_all x7 -> x0, waiting for transfers between devices: 20.4 us -> none  [the longest x5 14.1 us: exchange_in_order(): out = lax.all_to_all(out, axes[k], k, k, tiled=True)]
    dot_general x7 -> x0, matrix products: 17.6 us -> none  [the longest x3 12.4 us: on_device(): jnp.dot(normed, piece, preferred_element_type=jnp.float32)]
    gather x2 -> x0, local copies, waits for them, and re-layouts: 7.02 us -> none  [the longest x1 4.32 us: on_device(): vals = jnp.take(value_pages, page_table, axis=0)]
    convert_element_type x8 -> x1, other arithmetic: 6.31 us -> 0.94 us  [on_device(): return out.astype(jnp.bfloat16).reshape(ROWS, STEPS, HQ * HD)]
    unnamed x29 -> x2, local copies, waits for them, and re-layouts: 4.19 us -> 0.01 us
  transfers between devices with their start and end apart: 9 -> 0, of which waited for: 6 -> 0; matrix products, arithmetic and copies ran while one was open for 14% -> 0% of each run, Pallas kernels for 0% -> 0%
where the time goes in v1:
time: 85 us; the launch traced here: 84.6 us
  Pallas kernels  73.9 us (87%)
  local copies, waits for them, and re-layouts  6.5 us (8%)
  other arithmetic  4.17 us (5%)
    pallas_call x1, Pallas kernels, project(): pl.pallas_call(project_kernel, out_shape=(jax.ShapeDtypeStruct((8, 16, CO...  63.6 us
    pallas_call x1, Pallas kernels, attend(): pl.pallas_call(attend_kernel, out_shape=jax.ShapeDtypeStruct((ROWS, STEPS...  10.4 us

profile of v1, /device:TPU:1, one launch (start us, length us, event | category | flops | bytes accessed | tf_op | source)
XLA Modules:
  0.0 84.6 jit_solution(7509461194433335203)
XLA Ops:
  0.0 0.0 copy-start
  0.0 0.8 dynamic_slice.3
  0.8 0.7 tile.8
  1.5 0.1 tile.9
  1.5 0.7 tile.20
  2.2 0.1 tile.21
  2.3 0.7 pad_maximum_fusion
  3.0 1.1 %multiply_reduce_fusion = f32[48,4]{1,0:T(8,128)S(1)} fusion(bf16[48,4,512]{2,1,0:T(4,128)(2,1)} %param.12), kind=kLoop, calls=%fused_computation | loop fusion | flops 294720 | bytes 197376 | tf_op jit(solution)/shard_map/reduce_sum | solution.py:473
  4.1 0.1 reshape.92
  4.2 0.6 select_maximum_fusion.st_ref
  4.8 0.8 reshape.89
  5.7 0.8 reshape.90
  6.5 1.0 %copy.21 = f32[2,8,8,512]{3,2,0,1:T(8,128)S(1)} copy(f32[2,8,8,512]{3,2,1,0:T(8,128)} %bitcast.13) | data formatting | bytes 524288 | tf_op jit(solution)/shard_map/reshape | solution.py:468
  7.5 0.8 fusion.1.w_ref
  8.3 0.0 copy-done
  8.3 0.1 reshape.86
  8.4 0.7 reshape.87.x_ref
  9.1 63.6 %project.1 = (bf16[8,16,640]{2,1,0:T(8,128)(2,1)}, f32[16,8,128]{2,1,0:T(8,128)}) custom-call(bf16[192,512]{1,0:T(8,128)(2,1)} %reshape.87.x_ref, bf16[8,16,640]{2,1,0:T(8,128)(2,1)} %fusion.1.w_ref, f32[16,8,128]{2,1,0:T(8,128)} %select_maximum_fusion.st_ref), custom_call_target="tpu_custom_call" | custom-call | tf_op jit(solution)/shard_map/project/pallas_call | solution.py:297
  72.6 10.4 %attend.1 = f32[3,4,32,128]{3,2,1,0:T(8,128)} custom-call(s32[3]{0:T(128)} %len_ref.1, s32[3,8]{1,0:T(4,128)} %table_ref.1, bf16[8,16,640]{2,1,0:T(8,128)(2,1)} %get-tuple-element.7.qkv_ref, f32[16,8,128]{2,1,0:T(8,128)} %get-tuple-element.8.st_ref, bf16[16,4,128,128]{3,2,1,0:T(8,128)(2,1)} %kp_ref.1, bf16[16,4,128,128]{3,2,1,0:T(8,128)(2,1)} %vp_ref.1), custom_call_target="tpu_custom_call" | custom-call | tf_op jit(solution)/shard_map/attend/pallas_call | solution.py:433
  83.0 0.9 %convert_element_type.13 = bf16[3,4,32,128]{3,2,1,0:T(8,128)(2,1)S(1)} convert(f32[3,4,32,128]{3,2,1,0:T(8,128)} %attend.1) | non-fusion elementwise | flops 49152 | bytes 294912 | tf_op jit(solution)/shard_map/convert_element_type | solution.py:489
  84.0 0.7 reshape.93
  (5 shorter events, 0.1 us)
Async XLA Ops:
  0.0 8.3 %copy-start = (bf16[48,4,512]{2,1,0:T(4,128)(2,1)S(1)}, bf16[48,4,512]{2,1,0:T(4,128)(2,1)}, u32[]{:S(2)}) copy-start(bf16[48,4,512]{2,1,0:T(4,128)(2,1)} %param.12) | copy-start | bytes 589828

commit v2 on v1

v2 whole, which is shorter than its diff:
```python
import functools

import jax
import jax.numpy as jnp
from jax import lax
from jax.experimental import pallas as pl
from jax.experimental.pallas import tpu as pltpu
from jax.sharding import Mesh
from jax.sharding import PartitionSpec as P

HD = 128
HQ = 32
KVH = 4
GROUP = HQ // KVH
PAGE = 128
MOSTP = 8
STEPS = 4
ROWS = 3
OWN = ROWS * STEPS
D = 8192
EPS = 1e-06
THETA = 1000000.0
MESH = pl.DeviceIdType.MESH
AXES = ("yh", "z", "x", "yl", "c")
TP = ("x", "yl", "c")
REPLICA = ("yh", "z")
COLS = 640
KB = 512
BR = 192
RT = 96


def remote(src, dst, send, recv, where):
    return pltpu.make_async_remote_copy(
        src_ref=src, dst_ref=dst, send_sem=send, recv_sem=recv, device_id=where, device_id_type=MESH
    )


def column_of(row, shape):
    rows = lax.broadcasted_iota(jnp.int32, shape, 0)
    lanes = lax.broadcasted_iota(jnp.int32, shape, 1)
    return jnp.sum(
        jnp.where(rows == lanes, jnp.broadcast_to(row, shape), 0.0), axis=1, keepdims=True
    )


def prepare(
    block, h_ref, gain_ref, wq_ref, wk_ref, wv_ref, bq_ref, bk_ref, bv_ref, w_ref, st_ref
):
    row = gain_ref[pl.ds(block // 8, 1), :]
    rows = lax.broadcasted_iota(jnp.int32, (16, 128), 0)
    lanes = lax.broadcasted_iota(jnp.int32, (16, 128), 1)
    low = lanes < HD // 2
    gain = jnp.sum(
        jnp.where(lanes == rows + lax.rem(block, 8) * 16, jnp.broadcast_to(row, (16, 128)), 0.0),
        axis=1,
        keepdims=True,
    )
    for k in range(8):
        w_ref[k, :, 0:512] = (wq_ref[:, 512 * k : 512 * k + 512] * gain).astype(jnp.bfloat16)
        tiles = slice(HD * (k // 2), HD * (k // 2) + HD)
        tk, tv = wk_ref[:, tiles] * gain, wv_ref[:, tiles] * gain
        if k % 2 == 0:
            both = jnp.where(low, tk, pltpu.roll(tv, HD // 2, 1))
        else:
            both = jnp.where(low, pltpu.roll(tk, HD // 2, 1), tv)
        w_ref[k, :, 512:640] = both.astype(jnp.bfloat16)

    wide = h_ref[...].astype(jnp.float32)
    squares = jnp.sum(wide * wide, axis=1, keepdims=True)
    of_row = lax.broadcasted_iota(jnp.int32, (BR, 128), 0)
    of_lane = lax.broadcasted_iota(jnp.int32, (BR, 128), 1)
    spread = jnp.where(lax.rem(of_row, OWN) == of_lane, squares, 0.0)
    group = lax.broadcasted_iota(jnp.int32, (16, BR), 0)
    member = lax.broadcasted_iota(jnp.int32, (16, BR), 1)
    owner = jnp.where(member // OWN == group, 1.0, 0.0)
    per_owner = jnp.dot(
        owner, spread, preferred_element_type=jnp.float32, precision=lax.Precision.HIGHEST
    )
    for k in range(16):
        st_ref[k, 0:2, :] = bq_ref[...]
        st_ref[k, 2:3, 0:32] = bk_ref[...]
        st_ref[k, 3:4, 0:32] = bv_ref[...]
        st_ref[k, 4:5, :] = per_owner[k : k + 1, :]


def turns(len_ref, rope):
    rows = lax.broadcasted_iota(jnp.int32, (16, 128), 0)
    lanes = lax.broadcasted_iota(jnp.int32, (16, 128), 1)
    row_of = rows // STEPS
    length = jnp.where(row_of == 0, len_ref[0], jnp.where(row_of == 1, len_ref[1], len_ref[2]))
    position = (length + lax.rem(rows, STEPS)).astype(jnp.float32)
    pair = lax.rem(lanes, HD // 2).astype(jnp.float32)
    freq = jnp.power(THETA, -(pair * 2.0 / HD))
    angle = position * freq
    rope[0] = jnp.cos(angle)
    sin = jnp.sin(angle)
    rope[1] = jnp.where(lanes < HD // 2, -sin, sin)


def row_scale(strecv):
    squares = jnp.sum(strecv[:, 4, :], axis=0, keepdims=True)
    return lax.rsqrt(column_of(squares, (16, 128)) * (1.0 / D) + EPS)


def attend(kh, inv, len_ref, table_ref, qkv, st, rope, kpool, vpool, out_ref):
    rows = lax.broadcasted_iota(jnp.int32, (16, 128), 0)
    lanes = lax.broadcasted_iota(jnp.int32, (16, 128), 1)
    keep = rows < OWN
    low = lanes < HD // 2
    cos, sin = rope[0], rope[1]

    def made(total, bias):
        value = (total * inv + bias).astype(jnp.bfloat16).astype(jnp.float32)
        return jnp.where(keep, value, 0.0)

    def rotated(value):
        return (value * cos + pltpu.roll(value, HD // 2, 1) * sin).astype(jnp.bfloat16)

    def small_bias(at):
        lane = lax.broadcasted_iota(jnp.int32, (1, 128), 1)
        out = jnp.zeros((1, 128), jnp.float32)
        for i in range(4):
            piece = st[4 * kh + i, at : at + 1, :]
            if i:
                piece = pltpu.roll(piece, 32 * i, 1)
            out = jnp.where(lane // 32 == i, piece, out)
        return out

    heads = []
    for g in range(GROUP):
        i, a = g // 4, g % 4
        total = qkv[2 * kh + i, :, a * HD : (a + 1) * HD].astype(jnp.float32)
        bias = st[2 * (2 * kh + i) + a // 2, a % 2 : a % 2 + 1, :]
        heads.append(rotated(made(total, bias)))
    q_all = jnp.concatenate(heads, axis=0)
    t0 = qkv[2 * kh, :, 4 * HD : 5 * HD].astype(jnp.float32)
    t1 = qkv[2 * kh + 1, :, 4 * HD : 5 * HD].astype(jnp.float32)
    k_new = rotated(made(jnp.where(low, t0, pltpu.roll(t1, HD // 2, 1)), small_bias(2)))
    v_new = made(jnp.where(low, pltpu.roll(t0, HD // 2, 1), t1), small_bias(3))
    v_new = v_new.astype(jnp.bfloat16)

    sel_row = lax.broadcasted_iota(jnp.int32, (32, 128), 0)
    sel_col = lax.broadcasted_iota(jnp.int32, (32, 128), 1)
    new_row = lax.broadcasted_iota(jnp.int32, (32, 16), 0)
    new_col = lax.broadcasted_iota(jnp.int32, (32, 16), 1)
    spot = lax.broadcasted_iota(jnp.int32, (32, MOSTP * PAGE), 1)
    scale = 1.0 / HD**0.5
    contract = (((1,), (1,)), ((), ()))
    for r in range(ROWS):
        want = (sel_row // STEPS) * 16 + r * STEPS + lax.rem(sel_row, STEPS)
        pick = jnp.where(sel_col == want, 1.0, 0.0).astype(jnp.bfloat16)
        live = spot < len_ref[r]
        fresh_live = (new_col // STEPS == r) & (lax.rem(new_col, STEPS) <= lax.rem(new_row, STEPS))
        q = jnp.dot(pick, q_all, preferred_element_type=jnp.float32).astype(jnp.bfloat16)
        keys = jnp.concatenate([kpool[table_ref[r, m], kh] for m in range(MOSTP)], axis=0)
        vals = jnp.concatenate([vpool[table_ref[r, m], kh] for m in range(MOSTP)], axis=0)
        cache = lax.dot_general(q, keys, contract, preferred_element_type=jnp.float32) * scale
        cache = jnp.where(live, cache, -1e30)
        fresh = lax.dot_general(q, k_new, contract, preferred_element_type=jnp.float32) * scale
        fresh = jnp.where(fresh_live, fresh, -1e30)
        top = jnp.maximum(
            jnp.max(cache, axis=1, keepdims=True), jnp.max(fresh, axis=1, keepdims=True)
        )
        e_cache = jnp.where(live, jnp.exp(cache - top), 0.0)
        e_fresh = jnp.where(fresh_live, jnp.exp(fresh - top), 0.0)
        total = jnp.sum(e_cache, axis=1, keepdims=True) + jnp.sum(e_fresh, axis=1, keepdims=True)
        share = 1.0 / total
        w_cache = (e_cache * share).astype(jnp.bfloat16)
        w_fresh = (e_fresh * share).astype(jnp.bfloat16)
        out = jnp.dot(w_cache, vals, preferred_element_type=jnp.float32)
        out += jnp.dot(w_fresh, v_new, preferred_element_type=jnp.float32)
        for g in range(GROUP):
            at = pl.ds(pl.multiple_of(kh * GROUP * HD + g * HD, HD), HD)
            out_ref[r, :, at] = out[g * STEPS : (g + 1) * STEPS, :].astype(jnp.bfloat16)


def step_kernel(
    len_ref, table_ref, h_ref, gain_ref, wq_ref, wk_ref, wv_ref, bq_ref, bk_ref, bv_ref, kp_ref, vp_ref,
    out_ref,
    w_ref, st_ref, rope, kpool, vpool,
    xg, a1, wz, acc, dsend, drecv, rsend, rrecv, fin, ysend, yrecv, strecv,
    pools, xs, xr, a1s, a1r, a2s, a2r, ws, wr, sts, strs, d2s, d2r, rss, rrs, yss, yrs,
):
    yh, z, x, yl, c = (lax.axis_index(a) for a in AXES)
    y = yh * 2 + yl
    tp = x * 4 + yl * 2 + c
    zb = lax.rem(z // 2, 2)

    def at_y(k):
        return {"yh": k // 2, "yl": lax.rem(k, 2)}

    def at_tp(k):
        return {"x": k // 4, "yl": lax.rem(k // 2, 2), "c": lax.rem(k, 2)}

    def add(a, k, n):
        return lax.rem(a + (k + n) % n, n)

    pool_copies = (
        pltpu.make_async_copy(kp_ref, kpool, pools.at[0]),
        pltpu.make_async_copy(vp_ref, vpool, pools.at[1]),
    )
    for copy in pool_copies:
        copy.start()

    barrier = pltpu.get_barrier_semaphore()
    for d in range(1, 16):
        pl.semaphore_signal(barrier, inc=1, device_id=at_tp(add(tp, d, 16)), device_id_type=MESH)
    for d in range(1, 4):
        for k in range(4):
            pl.semaphore_signal(
                barrier,
                inc=1,
                device_id={"yh": add(yh, d, 4), "yl": k // 2, "c": k % 2},
                device_id_type=MESH,
            )
    for d in (1, -1):
        pl.semaphore_signal(barrier, inc=1, device_id={"z": add(z, d, 8)}, device_id_type=MESH)

    prepare(
        (yh * 8 + z) * 16 + tp, h_ref, gain_ref, wq_ref, wk_ref, wv_ref, bq_ref, bk_ref, bv_ref,
        w_ref, st_ref,
    )
    pl.semaphore_wait(barrier, 29)

    y_next = (at_y(add(y, 1, 8)), at_y(add(y, -1, 8)))
    z_next = ({"z": add(z, 1, 8)}, {"z": add(z, -1, 8)})

    def x_copy(s, h, way):
        o = add(y, -(s - 1) if way == 0 else s - 1, 8)
        rows = pl.ds(RT * h, RT)
        src = h_ref.at[rows] if s == 1 else xg.at[o, rows]
        return remote(
            src, xg.at[o, rows], xs.at[way, s - 1, h], xr.at[way, s - 1, h], y_next[way]
        )

    def x_wait(s, h, way):
        o = add(y, -s if way == 0 else s, 8)
        dst = xg.at[o, pl.ds(RT * h, RT)]
        remote(dst, dst, xs.at[way, s - 1, h], xr.at[way, s - 1, h], y_next[way]).wait_recv()

    def goes(s, h, way):
        return s <= 3 or (s == 4 and h == way)

    def origin_w(s, way):
        o = add(z, -s if way == 0 else s, 8)
        return o, lax.rem(o // 2, 2) == c, (o // 4) * 2 + lax.rem(o, 2)

    def w_copy(s, h, way):
        _, mine, j = origin_w(s - 1, way)
        part = wz.at[j, pl.ds(2 * h, 2)]
        return mine, remote(
            part, part, ws.at[way, s - 1, h], wr.at[way, s - 1, h], z_next[way]
        )

    def w_send(s, h, way):
        mine, copy = w_copy(s, h, way)

        @pl.when(mine)
        def _():
            copy.start()

    def w_step(s, h, way):
        _, mine, j = origin_w(s, way)
        part = wz.at[j, pl.ds(2 * h, 2)]

        @pl.when(mine)
        def _():
            remote(
                part, part, ws.at[way, s - 1, h], wr.at[way, s - 1, h], z_next[way]
            ).wait_recv()
            if goes(s + 1, h, way):
                w_copy(s + 1, h, way)[1].start()

    def x_step(s, h):
        for way in range(2):
            if goes(s, h, way):
                x_wait(s, h, way)
                if goes(s + 1, h, way):
                    x_copy(s + 1, h, way).start()

    def a1_copy(d):
        k = add(y, d, 8)
        return remote(w_ref.at[k], a1.at[y], a1s.at[d], a1r.at[y], at_y(k))

    for d in (4, 3, 5, 2, 6, 1, 7):
        a1_copy(d).start()
    for h in range(2):
        for way in range(2):
            x_copy(1, h, way).start()

    def st_copy(d):
        k = add(tp, d, 16)
        return remote(st_ref.at[k], strecv.at[tp], sts.at[d], strs.at[tp], at_tp(k))

    for d in range(1, 16):
        st_copy(d).start()
    a1[y] = w_ref[y]
    xg[y] = h_ref[...]
    strecv[tp] = st_ref[tp]
    turns(len_ref, rope)

    for d in range(1, 8):
        k = add(y, d, 8)
        remote(a1.at[k], a1.at[k], a1s.at[d], a1r.at[k], at_y(k)).wait_recv()

    own_j = (z // 4) * 2 + lax.rem(z, 2)

    def a2_copy(d):
        k = add(x, d, 4)
        return remote(
            a1.at[pl.ds(2 * k, 2)],
            wz.at[own_j, x, :, c],
            a2s.at[d],
            a2r.at[x * 2 + c],
            {"x": k, "c": zb},
        )

    for d in (2, 1, 3):
        a2_copy(d).start()

    @pl.when(zb != c)
    def _():
        a2_copy(0).start()

    @pl.when(zb == c)
    def _():
        wz[own_j, x, :, c] = a1[pl.ds(2 * x, 2)]

    x_step(1, 0)
    x_step(1, 1)

    @pl.when(zb == c)
    def _():
        for d in range(8):
            k = add(x * 2 + c, d, 8)
            kx, kc = k // 2, lax.rem(k, 2)
            dst = wz.at[own_j, kx, :, kc]
            if d > 0:
                remote(dst, dst, a2s.at[0], a2r.at[k], {"x": kx, "c": kc}).wait_recv()

    for h in range(2):
        for way in range(2):
            w_send(1, h, way)
    x_step(2, 0)
    x_step(2, 1)
    for s in range(1, 5):
        for h in range(2):
            for way in range(2):
                if goes(s, h, way):
                    w_step(s, h, way)
        if s == 1:
            x_step(3, 0)
            x_step(3, 1)
        if s == 2:
            x_step(4, 0)
            x_step(4, 1)

    def one_block(b, carry):
        total = jnp.zeros((BR, COLS), jnp.float32)
        for k in range(2):
            total += jnp.dot(
                xg[b * 2 + k],
                wz[2 * k : 2 * k + 2].reshape(KB, COLS),
                preferred_element_type=jnp.float32,
            )
        acc[b] = total
        return carry

    lax.fori_loop(0, 4, one_block, 0)

    def rows_for(kx, kc):
        at = pl.multiple_of((kx * 2 + kc) * 24, 8)
        return acc[:, pl.ds(at, 24), :].reshape(RT, COLS)

    oc = 1 - c
    order = (2, 1, 3, 0)

    def d_copy(d):
        return remote(dsend.at[d], drecv.at[d], d2s.at[d], d2r.at[d], {"c": oc})

    for d in order:
        dsend[d] = rows_for(add(x, d, 4), oc).astype(jnp.bfloat16)
        d_copy(d).start()

    def r_copy(d):
        k = add(x, d, 4)
        return remote(rsend.at[d], rrecv.at[x], rss.at[d], rrs.at[x], {"x": k})

    for d in order:
        d_copy(d).wait_recv()
        total = rows_for(add(x, d, 4), c) + drecv[d].astype(jnp.float32)
        if d:
            rsend[d] = total.astype(jnp.bfloat16)
            r_copy(d).start()
        else:
            fin[pl.ds(0, RT), :] = total
    fin[pl.ds(RT, 8), :] = jnp.zeros((8, COLS), jnp.float32)
    for d in (1, 3, 2):
        k = add(x, d, 4)
        remote(rrecv.at[k], rrecv.at[k], rss.at[d], rrs.at[k], {"x": k}).wait_recv()
        fin[pl.ds(0, RT), :] += rrecv[k].astype(jnp.float32)

    def y_copy(d, dc):
        k = add(yh, d, 4)
        kc = lax.rem(c + dc, 2)
        return remote(
            ysend.at[k, kc],
            yrecv.at[y],
            yss.at[d, dc],
            yrs.at[y],
            {"yh": k, "yl": c, "c": kc},
        )

    def y_each(act):
        for d in (0, 1, 3, 2):
            for dc in range(2):
                if d == 0 and dc == 0:

                    @pl.when(yl != c)
                    def _():
                        act(y_copy(0, 0))
                else:
                    act(y_copy(d, dc))

    for k in range(4):
        for kc in range(2):
            ysend[k, kc] = fin[pl.ds(24 * k + OWN * kc, 16), :].astype(jnp.bfloat16)
    y_each(lambda copy: copy.start())

    @pl.when(yl == c)
    def _():
        yrecv[y] = ysend[yh, c]

    for d in range(1, 16):
        k = add(tp, d, 16)
        remote(strecv.at[k], strecv.at[k], sts.at[d], strs.at[k], at_tp(k)).wait_recv()
    for copy in pool_copies:
        copy.wait()

    inv = row_scale(strecv)

    def one_group(d, carry):
        kh = lax.rem(yh + jnp.where(d == 2, 3, jnp.where(d == 3, 2, d)), 4)
        for i in range(2):
            k = kh * 2 + i

            @pl.when((k != y) | (yl != c))
            def _(k=k):
                remote(
                    yrecv.at[k], yrecv.at[k], yss.at[1, 0], yrs.at[k], {"yh": add(yh, 1, 4)}
                ).wait_recv()

        attend(kh, inv, len_ref, table_ref, yrecv, strecv, rope, kpool, vpool, out_ref)
        return carry

    lax.fori_loop(0, 4, one_group, 0)

    for d in range(1, 8):
        a1_copy(d).wait_send()
    y_each(lambda copy: copy.wait_send())
    for d in range(1, 16):
        st_copy(d).wait_send()
    for d in range(1, 4):
        a2_copy(d).wait_send()
        r_copy(d).wait_send()

    @pl.when(zb != c)
    def _():
        a2_copy(0).wait_send()

    for d in range(4):
        d_copy(d).wait_send()
    for s in range(1, 5):
        for h in range(2):
            for way in range(2):
                if goes(s, h, way):
                    x_copy(s, h, way).wait_send()
                    mine, copy = w_copy(s, h, way)

                    @pl.when(mine)
                    def _(copy=copy):
                        copy.wait_send()


def on_device(
    hidden,
    norm_gain,
    w_query,
    w_key,
    w_value,
    bias_query,
    bias_key,
    bias_value,
    key_pages,
    value_pages,
    kv_lengths,
    page_table,
):
    vm = pltpu.VMEM
    dma = pltpu.SemaphoreType.DMA
    bf = jnp.bfloat16
    f32 = jnp.float32
    return pl.pallas_call(
        step_kernel,
        out_shape=jax.ShapeDtypeStruct((ROWS, STEPS, HQ * HD), bf),
        in_specs=[pl.BlockSpec(memory_space=pltpu.SMEM)] * 2
        + [pl.BlockSpec(memory_space=vm)] * 8
        + [pl.BlockSpec(memory_space=pl.ANY)] * 2,
        out_specs=pl.BlockSpec(memory_space=vm),
        scratch_shapes=[
            vm((8, 16, COLS), bf),
            vm((16, 8, 128), f32),
            vm((2, 16, 128), f32),
            vm((16, KVH, PAGE, HD), bf),
            vm((16, KVH, PAGE, HD), bf),
            vm((8, BR, KB), bf),
            vm((8, 16, COLS), bf),
            vm((4, 4, 2, 2, 16, COLS), bf),
            vm((4, BR, COLS), f32),
            vm((4, RT, COLS), bf),
            vm((4, RT, COLS), bf),
            vm((4, RT, COLS), bf),
            vm((4, RT, COLS), bf),
            vm((RT + 8, COLS), f32),
            vm((4, 2, 16, COLS), bf),
            vm((8, 16, COLS), bf),
            vm((16, 8, 128), f32),
            dma((2,)),
            dma((2, 4, 2)), dma((2, 4, 2)),
            dma((8,)), dma((8,)),
            dma((4,)), dma((8,)),
            dma((2, 4, 2)), dma((2, 4, 2)),
            dma((16,)), dma((16,)),
            dma((4,)), dma((4,)),
            dma((4,)), dma((4,)),
            dma((4, 2)), dma((8,)),
        ],
        compiler_params=pltpu.CompilerParams(collective_id=0, has_side_effects=True),
        name="step",
    )(
        kv_lengths,
        page_table,
        hidden.reshape(BR, KB),
        norm_gain.reshape(D // 128, 128),
        w_query,
        w_key,
        w_value,
        bias_query.reshape(2, 128),
        bias_key.reshape(1, 32),
        bias_value.reshape(1, 32),
        key_pages,
        value_pages,
    )


def solution(mesh):
    split = Mesh(mesh.devices.reshape(4, 8, 4, 2, 2), AXES)
    both = REPLICA + TP
    in_specs = (
        P(REPLICA, None, TP),
        P(),
        P(both, None),
        P(both, None),
        P(both, None),
        P(TP),
        P(TP),
        P(TP),
        P(both, None, None, None),
        P(both, None, None, None),
        P(both),
        P(both, None),
    )
    return jax.shard_map(
        on_device, mesh=split, in_specs=in_specs, out_specs=P(both, None, None), check_vma=False
    )
```

time: 85 us -> 73 us (0.86)
  Pallas kernels: 73.9 us -> 69.6 us
  other arithmetic: 4.17 us -> 0 us
  local copies, waits for them, and re-layouts: 6.5 us -> 3.22 us
    pallas_call x2 -> x1, Pallas kernels: 73.9 us -> 69.6 us  [on_device(): pl.pallas_call(step_kernel, out_shape=jax.ShapeDtypeStruct((ROWS, STEPS,...]
    reshape x9 -> x1, local copies, waits for them, and re-layouts: 4.19 us -> 1.65 us  [on_device(): hidden.reshape(BR, KB)]
    unnamed x2 -> x1, local copies, waits for them, and re-layouts: 0.01 us -> 1.57 us
    another operation x4 -> x0, local copies, waits for them, and re-layouts: 1.48 us -> none  [the longest x2 0.74 us: on_device(): v_bias = jnp.where(place, jnp.tile(bias_value, 4), 0.0)]
    concatenate x2 -> x0, other arithmetic: 1.34 us -> none  [the longest x1 0.69 us: on_device(): jnp.concatenate([bias_query.reshape(2, 128), k_bias[None], v_bias[None]],...]
    reduce_sum x1 -> x0, other arithmetic: 1.1 us -> none  [on_device(): squares = jnp.sum(wide * wide, axis=2).reshape(16, 1, OWN)]
    convert_element_type x1 -> x0, other arithmetic: 0.94 us -> none  [on_device(): return out.astype(jnp.bfloat16).reshape(ROWS, STEPS, HQ * HD)]
where the time goes in v2:
time: 73 us; the launch traced here: 72.8 us
  Pallas kernels  69.6 us (95%)
  local copies, waits for them, and re-layouts  3.22 us (4%)
    pallas_call x1, Pallas kernels, on_device(): pl.pallas_call(step_kernel, out_shape=jax.ShapeDtypeStruct((ROWS, STEPS,...  69.6 us
    reshape x1, local copies, waits for them, and re-layouts, on_device(): hidden.reshape(BR, KB)  1.65 us
    unnamed x1, local copies, waits for them, and re-layouts  1.57 us

profile of v2, /device:TPU:1, one launch (start us, length us, event | category | flops | bytes accessed | tf_op | source)
XLA Modules:
  0.0 72.8 jit_solution(3934132840227268039)
XLA Ops:
  0.0 1.6 %reshape.15.h_ref = bf16[192,512]{1,0:T(8,128)(2,1)} reshape(bf16[48,4,512]{2,1,0:T(4,128)(2,1)} %param.12) | data formatting | bytes 393216 | tf_op jit(solution)/shard_map/reshape | solution.py:544
  1.6 69.6 %step.1 = bf16[3,4,4096]{2,1,0:T(4,128)(2,1)} custom-call(s32[3]{0:T(128)} %len_ref.1, s32[3,8]{1,0:T(4,128)} %table_ref.1, bf16[192,512]{1,0:T(8,128)(2,1)} %reshape.15.h_ref, f32[64,128]{1,0:T(8,128)} %bitcast.4, f32[16,4096]{1,0:T(8,128)} %wq_ref.1, f32[16,512]{1,0:T(8,128)} %wk_ref.1, f32[16,512]{1,0:T(8,128)} %wv_ref.1, f32[2,128]{1,0:T(2,128)} %bitcast.5, ...), custom_call_target="tpu_custom_call" | custom-call | tf_op jit(solution)/shard_map/step/pallas_call | solution.py:504
  71.3 1.6 %copy.14 = bf16[3,4,4096]{2,1,0:T(4,128)(2,1)} copy(bf16[3,4,4096]{2,1,0:T(4,128)(2,1)} %step.1) | data formatting | bytes 196608

commit v3 on v2

--- a/solution.py
+++ b/solution.py
@@ -44,9 +44,7 @@
     )
 
 
-def prepare(
-    block, h_ref, gain_ref, wq_ref, wk_ref, wv_ref, bq_ref, bk_ref, bv_ref, w_ref, st_ref
-):
+def cast_weights(block, gain_ref, wq_ref, wk_ref, wv_ref, w_ref):
     row = gain_ref[pl.ds(block // 8, 1), :]
     rows = lax.broadcasted_iota(jnp.int32, (16, 128), 0)
     lanes = lax.broadcasted_iota(jnp.int32, (16, 128), 1)
@@ -66,6 +64,8 @@
             both = jnp.where(low, pltpu.roll(tk, HD // 2, 1), tv)
         w_ref[k, :, 512:640] = both.astype(jnp.bfloat16)
 
+
+def fill_stats(h_ref, bq_ref, bk_ref, bv_ref, st_ref):
     wide = h_ref[...].astype(jnp.float32)
     squares = jnp.sum(wide * wide, axis=1, keepdims=True)
     of_row = lax.broadcasted_iota(jnp.int32, (BR, 128), 0)
@@ -172,15 +172,16 @@
         out += jnp.dot(w_fresh, v_new, preferred_element_type=jnp.float32)
         for g in range(GROUP):
             at = pl.ds(pl.multiple_of(kh * GROUP * HD + g * HD, HD), HD)
-            out_ref[r, :, at] = out[g * STEPS : (g + 1) * STEPS, :].astype(jnp.bfloat16)
+            out_ref[r, :, at] = out[g * STEPS : (g + 1) * STEPS, :]
 
 
 def step_kernel(
-    len_ref, table_ref, h_ref, gain_ref, wq_ref, wk_ref, wv_ref, bq_ref, bk_ref, bv_ref, kp_ref, vp_ref,
+    len_ref, table_ref, h_hbm, gain_hbm, wq_hbm, wk_hbm, wv_hbm, bq_hbm, bk_hbm, bv_hbm, kp_ref, vp_ref,
     out_ref,
+    raw, gain_ref, wq_ref, wk_ref, wv_ref, bq_ref, bk_ref, bv_ref, h_ref,
     w_ref, st_ref, rope, kpool, vpool,
     xg, a1, wz, acc, dsend, drecv, rsend, rrecv, fin, ysend, yrecv, strecv,
-    pools, xs, xr, a1s, a1r, a2s, a2r, ws, wr, sts, strs, d2s, d2r, rss, rrs, yss, yrs,
+    ins, pools, xs, xr, a1s, a1r, a2s, a2r, ws, wr, sts, strs, d2s, d2r, rss, rrs, yss, yrs,
 ):
     yh, z, x, yl, c = (lax.axis_index(a) for a in AXES)
     y = yh * 2 + yl
@@ -200,7 +201,16 @@
         pltpu.make_async_copy(kp_ref, kpool, pools.at[0]),
         pltpu.make_async_copy(vp_ref, vpool, pools.at[1]),
     )
-    for copy in pool_copies:
+    in_copies = [
+        pltpu.make_async_copy(src, dst, ins.at[k])
+        for k, (src, dst) in enumerate(
+            (
+                (wq_hbm, wq_ref), (wk_hbm, wk_ref), (wv_hbm, wv_ref), (gain_hbm, gain_ref),
+                (h_hbm, raw), (bq_hbm, bq_ref), (bk_hbm, bk_ref), (bv_hbm, bv_ref),
+            )
+        )
+    ]
+    for copy in in_copies:
         copy.start()
 
     barrier = pltpu.get_barrier_semaphore()
@@ -217,11 +227,14 @@
     for d in (1, -1):
         pl.semaphore_signal(barrier, inc=1, device_id={"z": add(z, d, 8)}, device_id_type=MESH)
 
-    prepare(
-        (yh * 8 + z) * 16 + tp, h_ref, gain_ref, wq_ref, wk_ref, wv_ref, bq_ref, bk_ref, bv_ref,
-        w_ref, st_ref,
-    )
+    for copy in in_copies[:4]:
+        copy.wait()
+    cast_weights((yh * 8 + z) * 16 + tp, gain_ref, wq_ref, wk_ref, wv_ref, w_ref)
+    in_copies[4].wait()
+    h_ref[...] = raw[...].reshape(BR, KB)
     pl.semaphore_wait(barrier, 29)
+    for copy in pool_copies:
+        copy.start()
 
     y_next = (at_y(add(y, 1, 8)), at_y(add(y, -1, 8)))
     z_next = ({"z": add(z, 1, 8)}, {"z": add(z, -1, 8)})
@@ -242,35 +255,33 @@
     def goes(s, h, way):
         return s <= 3 or (s == 4 and h == way)
 
+    turn = (0, 1, 3, 2)
+
+    def goes_w(s, q, way):
+        return goes(s, q // 2, way)
+
     def origin_w(s, way):
         o = add(z, -s if way == 0 else s, 8)
         return o, lax.rem(o // 2, 2) == c, (o // 4) * 2 + lax.rem(o, 2)
 
-    def w_copy(s, h, way):
+    def w_copy(s, q, way):
         _, mine, j = origin_w(s - 1, way)
-        part = wz.at[j, pl.ds(2 * h, 2)]
+        part = wz.at[j, add(x, turn[q], 4)]
         return mine, remote(
-            part, part, ws.at[way, s - 1, h], wr.at[way, s - 1, h], z_next[way]
-        )
-
-    def w_send(s, h, way):
-        mine, copy = w_copy(s, h, way)
-
-        @pl.when(mine)
-        def _():
-            copy.start()
-
-    def w_step(s, h, way):
+            part, part, ws.at[way, s - 1, q], wr.at[way, s - 1, q], z_next[way]
+        )
+
+    def w_step(s, q, way):
         _, mine, j = origin_w(s, way)
-        part = wz.at[j, pl.ds(2 * h, 2)]
+        part = wz.at[j, add(x, turn[q], 4)]
 
         @pl.when(mine)
         def _():
             remote(
-                part, part, ws.at[way, s - 1, h], wr.at[way, s - 1, h], z_next[way]
+                part, part, ws.at[way, s - 1, q], wr.at[way, s - 1, q], z_next[way]
             ).wait_recv()
-            if goes(s + 1, h, way):
-                w_copy(s + 1, h, way)[1].start()
+            if goes_w(s + 1, q, way):
+                w_copy(s + 1, q, way)[1].start()
 
     def x_step(s, h):
         for way in range(2):
@@ -293,6 +304,9 @@
         k = add(tp, d, 16)
         return remote(st_ref.at[k], strecv.at[tp], sts.at[d], strs.at[tp], at_tp(k))
 
+    for copy in in_copies[5:]:
+        copy.wait()
+    fill_stats(h_ref, bq_ref, bk_ref, bv_ref, st_ref)
     for d in range(1, 16):
         st_copy(d).start()
     a1[y] = w_ref[y]
@@ -332,29 +346,27 @@
 
     @pl.when(zb == c)
     def _():
-        for d in range(8):
-            k = add(x * 2 + c, d, 8)
-            kx, kc = k // 2, lax.rem(k, 2)
-            dst = wz.at[own_j, kx, :, kc]
-            if d > 0:
+        for q in range(4):
+            kx = add(x, turn[q], 4)
+            for kc in (c, 1 - c):
+                if q == 0 and kc is c:
+                    continue
+                dst = wz.at[own_j, kx, :, kc]
+                k = kx * 2 + kc
                 remote(dst, dst, a2s.at[0], a2r.at[k], {"x": kx, "c": kc}).wait_recv()
-
-    for h in range(2):
-        for way in range(2):
-            w_send(1, h, way)
+            for way in range(2):
+                w_copy(1, q, way)[1].start()
+
     x_step(2, 0)
     x_step(2, 1)
     for s in range(1, 5):
-        for h in range(2):
+        for q in range(4):
             for way in range(2):
-                if goes(s, h, way):
-                    w_step(s, h, way)
-        if s == 1:
-            x_step(3, 0)
-            x_step(3, 1)
-        if s == 2:
-            x_step(4, 0)
-            x_step(4, 1)
+                if goes_w(s, q, way):
+                    w_step(s, q, way)
+        if s <= 2:
+            x_step(s + 2, 0)
+            x_step(s + 2, 1)
 
     def one_block(b, carry):
         total = jnp.zeros((BR, COLS), jnp.float32)
@@ -367,39 +379,60 @@
         acc[b] = total
         return carry
 
-    lax.fori_loop(0, 4, one_block, 0)
-
-    def rows_for(kx, kc):
+    oc = 1 - c
+    HR = RT // 2
+
+    def rows_for(half, kx, kc):
         at = pl.multiple_of((kx * 2 + kc) * 24, 8)
-        return acc[:, pl.ds(at, 24), :].reshape(RT, COLS)
-
-    oc = 1 - c
+        return acc[2 * half : 2 * half + 2, pl.ds(at, 24), :].reshape(HR, COLS)
+
     order = (2, 1, 3, 0)
 
-    def d_copy(d):
-        return remote(dsend.at[d], drecv.at[d], d2s.at[d], d2r.at[d], {"c": oc})
-
-    for d in order:
-        dsend[d] = rows_for(add(x, d, 4), oc).astype(jnp.bfloat16)
-        d_copy(d).start()
-
-    def r_copy(d):
-        k = add(x, d, 4)
-        return remote(rsend.at[d], rrecv.at[x], rss.at[d], rrs.at[x], {"x": k})
-
-    for d in order:
-        d_copy(d).wait_recv()
-        total = rows_for(add(x, d, 4), c) + drecv[d].astype(jnp.float32)
-        if d:
-            rsend[d] = total.astype(jnp.bfloat16)
-            r_copy(d).start()
-        else:
-            fin[pl.ds(0, RT), :] = total
+    def d_copy(half, d):
+        return remote(
+            dsend.at[half, d], drecv.at[half, d], d2s.at[half, d], d2r.at[half, d], {"c": oc}
+        )
+
+    for half in range(2):
+        lax.fori_loop(2 * half, 2 * half + 2, one_block, 0)
+        for d in order:
+            dsend[half, d] = rows_for(half, add(x, d, 4), oc).astype(jnp.bfloat16)
+            d_copy(half, d).start()
+
+    def both_cores(half, d):
+        d_copy(half, d).wait_recv()
+        return rows_for(half, add(x, d, 4), c) + drecv[half, d].astype(jnp.float32)
+
+    x_next = ({"x": add(x, 1, 4)}, {"x": add(x, -1, 4)})
+
+    def r_copy(kind, half):
+        way = half if kind == 0 else (1 - half if kind == 1 else half)
+        return remote(
+            rsend.at[kind, half], rrecv.at[kind, half], rss.at[kind, half], rrs.at[kind, half],
+            x_next[way],
+        )
+
+    for half in range(2):
+        rsend[0, half] = both_cores(half, 2).astype(jnp.bfloat16)
+        r_copy(0, half).start()
+        rsend[1, half] = both_cores(half, 3 if half == 0 else 1).astype(jnp.bfloat16)
+        r_copy(1, half).start()
+    for half in range(2):
+        fin[pl.ds(half * HR, HR), :] = both_cores(half, 1 if half == 0 else 3)
+    for half in range(2):
+        r_copy(0, half).wait_recv()
+        total = fin[pl.ds(half * HR, HR), :] + rrecv[0, half].astype(jnp.float32)
+        rsend[2, half] = total.astype(jnp.bfloat16)
+        r_copy(2, half).start()
     fin[pl.ds(RT, 8), :] = jnp.zeros((8, COLS), jnp.float32)
-    for d in (1, 3, 2):
-        k = add(x, d, 4)
-        remote(rrecv.at[k], rrecv.at[k], rss.at[d], rrs.at[k], {"x": k}).wait_recv()
-        fin[pl.ds(0, RT), :] += rrecv[k].astype(jnp.float32)
+    for half in range(2):
+        fin[pl.ds(half * HR, HR), :] = both_cores(half, 0)
+    for half in range(2):
+        r_copy(1, half).wait_recv()
+        fin[pl.ds(half * HR, HR), :] += rrecv[1, half].astype(jnp.float32)
+    for half in range(2):
+        r_copy(2, half).wait_recv()
+        fin[pl.ds(half * HR, HR), :] += rrecv[2, half].astype(jnp.float32)
 
     def y_copy(d, dc):
         k = add(yh, d, 4)
@@ -463,20 +496,26 @@
         st_copy(d).wait_send()
     for d in range(1, 4):
         a2_copy(d).wait_send()
-        r_copy(d).wait_send()
 
     @pl.when(zb != c)
     def _():
         a2_copy(0).wait_send()
 
-    for d in range(4):
-        d_copy(d).wait_send()
+    for half in range(2):
+        for d in range(4):
+            d_copy(half, d).wait_send()
+        for kind in range(3):
+            r_copy(kind, half).wait_send()
     for s in range(1, 5):
         for h in range(2):
             for way in range(2):
                 if goes(s, h, way):
                     x_copy(s, h, way).wait_send()
-                    mine, copy = w_copy(s, h, way)
+    for s in range(1, 5):
+        for q in range(4):
+            for way in range(2):
+                if goes_w(s, q, way):
+                    mine, copy = w_copy(s, q, way)
 
                     @pl.when(mine)
                     def _(copy=copy):
@@ -501,14 +540,22 @@
     dma = pltpu.SemaphoreType.DMA
     bf = jnp.bfloat16
     f32 = jnp.float32
-    return pl.pallas_call(
+    out = pl.pallas_call(
         step_kernel,
-        out_shape=jax.ShapeDtypeStruct((ROWS, STEPS, HQ * HD), bf),
+        out_shape=jax.ShapeDtypeStruct((ROWS, STEPS, HQ * HD), f32),
         in_specs=[pl.BlockSpec(memory_space=pltpu.SMEM)] * 2
-        + [pl.BlockSpec(memory_space=vm)] * 8
-        + [pl.BlockSpec(memory_space=pl.ANY)] * 2,
+        + [pl.BlockSpec(memory_space=pl.ANY)] * 10,
         out_specs=pl.BlockSpec(memory_space=vm),
         scratch_shapes=[
+            vm((ROWS * 16, STEPS, KB), bf),
+            vm((D // 128, 128), f32),
+            vm((16, HQ * HD), f32),
+            vm((16, KVH * HD), f32),
+            vm((16, KVH * HD), f32),
+            vm((2, 128), f32),
+            vm((1, 32), f32),
+            vm((1, 32), f32),
+            vm((BR, KB), bf),
             vm((8, 16, COLS), bf),
             vm((16, 8, 128), f32),
             vm((2, 16, 128), f32),
@@ -518,22 +565,22 @@
             vm((8, 16, COLS), bf),
             vm((4, 4, 2, 2, 16, COLS), bf),
             vm((4, BR, COLS), f32),
-            vm((4, RT, COLS), bf),
-            vm((4, RT, COLS), bf),
-            vm((4, RT, COLS), bf),
-            vm((4, RT, COLS), bf),
+            vm((2, 4, RT // 2, COLS), bf),
+            vm((2, 4, RT // 2, COLS), bf),
+            vm((3, 2, RT // 2, COLS), bf),
+            vm((3, 2, RT // 2, COLS), bf),
             vm((RT + 8, COLS), f32),
             vm((4, 2, 16, COLS), bf),
             vm((8, 16, COLS), bf),
             vm((16, 8, 128), f32),
-            dma((2,)),
+            dma((8,)), dma((2,)),
             dma((2, 4, 2)), dma((2, 4, 2)),
             dma((8,)), dma((8,)),
             dma((4,)), dma((8,)),
-            dma((2, 4, 2)), dma((2, 4, 2)),
+            dma((2, 4, 4)), dma((2, 4, 4)),
             dma((16,)), dma((16,)),
-            dma((4,)), dma((4,)),
-            dma((4,)), dma((4,)),
+            dma((2, 4)), dma((2, 4)),
+            dma((3, 2)), dma((3, 2)),
             dma((4, 2)), dma((8,)),
         ],
         compiler_params=pltpu.CompilerParams(collective_id=0, has_side_effects=True),
@@ -541,7 +588,7 @@
     )(
         kv_lengths,
         page_table,
-        hidden.reshape(BR, KB),
+        hidden,
         norm_gain.reshape(D // 128, 128),
         w_query,
         w_key,
@@ -552,6 +599,7 @@
         key_pages,
         value_pages,
     )
+    return out.astype(bf)
 
 
 def solution(mesh):

time: 73 us -> 70 us (0.959)
  local copies, waits for them, and re-layouts: 3.22 us -> 0 us
  other arithmetic: 0 us -> 1.6 us
  Pallas kernels: 69.6 us -> 68.3 us
    reshape x1 -> x0, local copies, waits for them, and re-layouts: 1.65 us -> none  [on_device(): hidden.reshape(BR, KB)]
    convert_element_type x0 -> x1, other arithmetic: none -> 1.6 us  [on_device(): return out.astype(bf)]
    unnamed x1 -> x0, local copies, waits for them, and re-layouts: 1.57 us -> none
    pallas_call x1, Pallas kernels: 69.6 us -> 68.3 us  [on_device(): pl.pallas_call(step_kernel, out_shape=jax.ShapeDtypeStruct((ROWS, STEPS,...]
where the time goes in v3:
time: 70 us; the launch traced here: 69.9 us
  Pallas kernels  68.3 us (98%)
  other arithmetic  1.6 us (2%)
    pallas_call x1, Pallas kernels, on_device(): pl.pallas_call(step_kernel, out_shape=jax.ShapeDtypeStruct((ROWS, STEPS,...  68.3 us
    convert_element_type x1, other arithmetic, on_device(): return out.astype(bf)  1.6 us

profile of v3, /device:TPU:1, one launch (start us, length us, event | category | flops | bytes accessed | tf_op | source)
XLA Modules:
  0.0 69.9 jit_solution(14568035489063677267)
XLA Ops:
  0.0 68.3 %step.1 = f32[3,4,4096]{2,1,0:T(4,128)} custom-call(s32[3]{0:T(128)} %len_ref.1, s32[3,8]{1,0:T(4,128)} %table_ref.1, bf16[48,4,512]{2,1,0:T(4,128)(2,1)} %h_hbm.1, f32[64,128]{1,0:T(8,128)} %bitcast.4, f32[16,4096]{1,0:T(8,128)} %wq_hbm.1, f32[16,512]{1,0:T(8,128)} %wk_hbm.1, f32[16,512]{1,0:T(8,128)} %wv_hbm.1, f32[2,128]{1,0:T(2,128)} %bitcast.5, ...), custom_call_target="tpu_custom_call" | custom-call | tf_op jit(solution)/shard_map/step/pallas_call | solution.py:543
  68.3 1.6 %convert_element_type.3 = bf16[3,4,4096]{2,1,0:T(4,128)(2,1)} convert(f32[3,4,4096]{2,1,0:T(4,128)} %step.1) | non-fusion elementwise | flops 49152 | bytes 294912 | tf_op jit(solution)/shard_map/convert_element_type | solution.py:602

commit v4 on v3

--- a/solution.py
+++ b/solution.py
@@ -27,6 +27,7 @@
 COLS = 640
 KB = 512
 BR = 192
+KEYS = MOSTP * PAGE + 128
 RT = 96
 
 
@@ -103,12 +104,13 @@
     return lax.rsqrt(column_of(squares, (16, 128)) * (1.0 / D) + EPS)
 
 
-def attend(kh, inv, len_ref, table_ref, qkv, st, rope, kpool, vpool, out_ref):
+def attend(groups, inv, len_ref, table_ref, qkv, st, rope, kpool, vpool, score, out_ref):
     rows = lax.broadcasted_iota(jnp.int32, (16, 128), 0)
     lanes = lax.broadcasted_iota(jnp.int32, (16, 128), 1)
     keep = rows < OWN
     low = lanes < HD // 2
     cos, sin = rope[0], rope[1]
+    nothing = jnp.zeros((112, HD), jnp.bfloat16)
 
     def made(total, bias):
         value = (total * inv + bias).astype(jnp.bfloat16).astype(jnp.float32)
@@ -117,7 +119,7 @@
     def rotated(value):
         return (value * cos + pltpu.roll(value, HD // 2, 1) * sin).astype(jnp.bfloat16)
 
-    def small_bias(at):
+    def small_bias(kh, at):
         lane = lax.broadcasted_iota(jnp.int32, (1, 128), 1)
         out = jnp.zeros((1, 128), jnp.float32)
         for i in range(4):
@@ -127,61 +129,75 @@
             out = jnp.where(lane // 32 == i, piece, out)
         return out
 
-    heads = []
-    for g in range(GROUP):
-        i, a = g // 4, g % 4
-        total = qkv[2 * kh + i, :, a * HD : (a + 1) * HD].astype(jnp.float32)
-        bias = st[2 * (2 * kh + i) + a // 2, a % 2 : a % 2 + 1, :]
-        heads.append(rotated(made(total, bias)))
-    q_all = jnp.concatenate(heads, axis=0)
-    t0 = qkv[2 * kh, :, 4 * HD : 5 * HD].astype(jnp.float32)
-    t1 = qkv[2 * kh + 1, :, 4 * HD : 5 * HD].astype(jnp.float32)
-    k_new = rotated(made(jnp.where(low, t0, pltpu.roll(t1, HD // 2, 1)), small_bias(2)))
-    v_new = made(jnp.where(low, pltpu.roll(t0, HD // 2, 1), t1), small_bias(3))
-    v_new = v_new.astype(jnp.bfloat16)
-
     sel_row = lax.broadcasted_iota(jnp.int32, (32, 128), 0)
     sel_col = lax.broadcasted_iota(jnp.int32, (32, 128), 1)
-    new_row = lax.broadcasted_iota(jnp.int32, (32, 16), 0)
-    new_col = lax.broadcasted_iota(jnp.int32, (32, 16), 1)
     spot = lax.broadcasted_iota(jnp.int32, (32, MOSTP * PAGE), 1)
     scale = 1.0 / HD**0.5
     contract = (((1,), (1,)), ((), ()))
-    for r in range(ROWS):
+    chains = [(n, kh, r) for n, kh in enumerate(groups) for r in range(ROWS)]
+    made_of = []
+    for kh in groups:
+        heads = []
+        for g in range(GROUP):
+            i, a = g // 4, g % 4
+            total = qkv[2 * kh + i, :, a * HD : (a + 1) * HD].astype(jnp.float32)
+            bias = st[2 * (2 * kh + i) + a // 2, a % 2 : a % 2 + 1, :]
+            heads.append(rotated(made(total, bias)))
+        t0 = qkv[2 * kh, :, 4 * HD : 5 * HD].astype(jnp.float32)
+        t1 = qkv[2 * kh + 1, :, 4 * HD : 5 * HD].astype(jnp.float32)
+        k_new = rotated(made(jnp.where(low, t0, pltpu.roll(t1, HD // 2, 1)), small_bias(kh, 2)))
+        v_new = made(jnp.where(low, pltpu.roll(t0, HD // 2, 1), t1), small_bias(kh, 3))
+        made_of.append((jnp.concatenate(heads, axis=0), k_new, v_new.astype(jnp.bfloat16)))
+
+    queries = []
+    for n, kh, r in chains:
         want = (sel_row // STEPS) * 16 + r * STEPS + lax.rem(sel_row, STEPS)
         pick = jnp.where(sel_col == want, 1.0, 0.0).astype(jnp.bfloat16)
-        live = spot < len_ref[r]
-        fresh_live = (new_col // STEPS == r) & (lax.rem(new_col, STEPS) <= lax.rem(new_row, STEPS))
-        q = jnp.dot(pick, q_all, preferred_element_type=jnp.float32).astype(jnp.bfloat16)
-        keys = jnp.concatenate([kpool[table_ref[r, m], kh] for m in range(MOSTP)], axis=0)
-        vals = jnp.concatenate([vpool[table_ref[r, m], kh] for m in range(MOSTP)], axis=0)
-        cache = lax.dot_general(q, keys, contract, preferred_element_type=jnp.float32) * scale
-        cache = jnp.where(live, cache, -1e30)
-        fresh = lax.dot_general(q, k_new, contract, preferred_element_type=jnp.float32) * scale
-        fresh = jnp.where(fresh_live, fresh, -1e30)
-        top = jnp.maximum(
-            jnp.max(cache, axis=1, keepdims=True), jnp.max(fresh, axis=1, keepdims=True)
-        )
-        e_cache = jnp.where(live, jnp.exp(cache - top), 0.0)
-        e_fresh = jnp.where(fresh_live, jnp.exp(fresh - top), 0.0)
-        total = jnp.sum(e_cache, axis=1, keepdims=True) + jnp.sum(e_fresh, axis=1, keepdims=True)
-        share = 1.0 / total
-        w_cache = (e_cache * share).astype(jnp.bfloat16)
-        w_fresh = (e_fresh * share).astype(jnp.bfloat16)
-        out = jnp.dot(w_cache, vals, preferred_element_type=jnp.float32)
-        out += jnp.dot(w_fresh, v_new, preferred_element_type=jnp.float32)
+        q = jnp.dot(pick, made_of[n][0], preferred_element_type=jnp.float32)
+        queries.append(q.astype(jnp.bfloat16))
+    tops = []
+    for (n, kh, r), q in zip(chains, queries):
+        keys = jnp.concatenate(
+            [kpool[table_ref[r, m], kh] for m in range(MOSTP)] + [made_of[n][1], nothing], axis=0
+        )
+        raw = lax.dot_general(q, keys, contract, preferred_element_type=jnp.float32)
+        cache = jnp.where(spot < len_ref[r], raw[:, : MOSTP * PAGE], -1e30)
+        fresh_live = (
+            (sel_col < OWN)
+            & (sel_col // STEPS == r)
+            & (lax.rem(sel_col, STEPS) <= lax.rem(sel_row, STEPS))
+        )
+        fresh = jnp.where(fresh_live, raw[:, MOSTP * PAGE :], -1e30)
+        score[n * ROWS + r, :, 0 : MOSTP * PAGE] = cache
+        score[n * ROWS + r, :, MOSTP * PAGE : KEYS] = fresh
+        tops.append(
+            jnp.maximum(
+                jnp.max(cache, axis=1, keepdims=True), jnp.max(fresh, axis=1, keepdims=True)
+            )
+        )
+    results = []
+    for (n, kh, r), top in zip(chains, tops):
+        weight = jnp.exp((score[n * ROWS + r] - top) * scale)
+        total = jnp.sum(weight, axis=1, keepdims=True)
+        vals = jnp.concatenate(
+            [vpool[table_ref[r, m], kh] for m in range(MOSTP)] + [made_of[n][2], nothing], axis=0
+        )
+        out = jnp.dot(weight.astype(jnp.bfloat16), vals, preferred_element_type=jnp.float32)
+        results.append((out, total))
+    for (n, kh, r), (out, total) in zip(chains, results):
+        out = (out / total).astype(jnp.bfloat16)
         for g in range(GROUP):
             at = pl.ds(pl.multiple_of(kh * GROUP * HD + g * HD, HD), HD)
             out_ref[r, :, at] = out[g * STEPS : (g + 1) * STEPS, :]
 
 
 def step_kernel(
-    len_ref, table_ref, h_hbm, gain_hbm, wq_hbm, wk_hbm, wv_hbm, bq_hbm, bk_hbm, bv_hbm, kp_ref, vp_ref,
-    out_ref,
-    raw, gain_ref, wq_ref, wk_ref, wv_ref, bq_ref, bk_ref, bv_ref, h_ref,
+    len_hbm, table_hbm, h_hbm, gain_hbm, wq_hbm, wk_hbm, wv_hbm, bq_hbm, bk_hbm, bv_hbm, kp_ref, vp_ref,
+    out_hbm,
+    len_ref, table_ref, out_ref, score, raw, gain_ref, wq_ref, wk_ref, wv_ref, bq_ref, bk_ref, bv_ref, h_ref,
     w_ref, st_ref, rope, kpool, vpool,
-    xg, a1, wz, acc, dsend, drecv, rsend, rrecv, fin, ysend, yrecv, strecv,
-    ins, pools, xs, xr, a1s, a1r, a2s, a2r, ws, wr, sts, strs, d2s, d2r, rss, rrs, yss, yrs,
+    xg, wz, acc, dsend, drecv, rsend, rrecv, fin, ysend, yrecv, strecv,
+    ins, outs, pools, xs, xr, a1s, a1r, ws, wr, sts, strs, d2s, d2r, rss, rrs, yss, yrs,
 ):
     yh, z, x, yl, c = (lax.axis_index(a) for a in AXES)
     y = yh * 2 + yl
@@ -195,7 +211,7 @@
         return {"x": k // 4, "yl": lax.rem(k // 2, 2), "c": lax.rem(k, 2)}
 
     def add(a, k, n):
-        return lax.rem(a + (k + n) % n, n)
+        return lax.rem(a + lax.rem(k + n, n), n)
 
     pool_copies = (
         pltpu.make_async_copy(kp_ref, kpool, pools.at[0]),
@@ -207,6 +223,7 @@
             (
                 (wq_hbm, wq_ref), (wk_hbm, wk_ref), (wv_hbm, wv_ref), (gain_hbm, gain_ref),
                 (h_hbm, raw), (bq_hbm, bq_ref), (bk_hbm, bk_ref), (bv_hbm, bv_ref),
+                (len_hbm, len_ref), (table_hbm, table_ref),
             )
         )
     ]
@@ -214,16 +231,21 @@
         copy.start()
 
     barrier = pltpu.get_barrier_semaphore()
-    for d in range(1, 16):
-        pl.semaphore_signal(barrier, inc=1, device_id=at_tp(add(tp, d, 16)), device_id_type=MESH)
-    for d in range(1, 4):
-        for k in range(4):
-            pl.semaphore_signal(
-                barrier,
-                inc=1,
-                device_id={"yh": add(yh, d, 4), "yl": k // 2, "c": k % 2},
-                device_id_type=MESH,
-            )
+    near_x = [add(x, d, 4) for d in range(4)]
+    near_yh = [add(yh, d, 4) for d in range(4)]
+    near_yl, near_c = (yl, 1 - yl), (c, 1 - c)
+    for k in range(1, 64):
+        pl.semaphore_signal(
+            barrier,
+            inc=1,
+            device_id={
+                "yh": near_yh[k // 16],
+                "x": near_x[k // 4 % 4],
+                "yl": near_yl[k // 2 % 2],
+                "c": near_c[k % 2],
+            },
+            device_id_type=MESH,
+        )
     for d in (1, -1):
         pl.semaphore_signal(barrier, inc=1, device_id={"z": add(z, d, 8)}, device_id_type=MESH)
 
@@ -232,7 +254,7 @@
     cast_weights((yh * 8 + z) * 16 + tp, gain_ref, wq_ref, wk_ref, wv_ref, w_ref)
     in_copies[4].wait()
     h_ref[...] = raw[...].reshape(BR, KB)
-    pl.semaphore_wait(barrier, 29)
+    pl.semaphore_wait(barrier, 65)
     for copy in pool_copies:
         copy.start()
 
@@ -244,13 +266,13 @@
         rows = pl.ds(RT * h, RT)
         src = h_ref.at[rows] if s == 1 else xg.at[o, rows]
         return remote(
-            src, xg.at[o, rows], xs.at[way, s - 1, h], xr.at[way, s - 1, h], y_next[way]
+            src, xg.at[o, rows], xs.at[0], xr.at[way, s - 1, h], y_next[way]
         )
 
     def x_wait(s, h, way):
         o = add(y, -s if way == 0 else s, 8)
         dst = xg.at[o, pl.ds(RT * h, RT)]
-        remote(dst, dst, xs.at[way, s - 1, h], xr.at[way, s - 1, h], y_next[way]).wait_recv()
+        remote(dst, dst, xs.at[0], xr.at[way, s - 1, h], y_next[way]).wait_recv()
 
     def goes(s, h, way):
         return s <= 3 or (s == 4 and h == way)
@@ -290,94 +312,113 @@
                 if goes(s + 1, h, way):
                     x_copy(s + 1, h, way).start()
 
+    own_j = (z // 4) * 2 + lax.rem(z, 2)
+
     def a1_copy(d):
         k = add(y, d, 8)
-        return remote(w_ref.at[k], a1.at[y], a1s.at[d], a1r.at[y], at_y(k))
-
+        return remote(
+            w_ref.at[k],
+            wz.at[own_j, x, yl, c],
+            a1s.at[d],
+            a1r.at[tp],
+            {"x": yh, "yh": k // 2, "yl": lax.rem(k, 2), "c": zb},
+        )
+
+    at_home = (x == yh) & (zb == c)
     for d in (4, 3, 5, 2, 6, 1, 7):
         a1_copy(d).start()
+
+    @pl.when(jnp.logical_not(at_home))
+    def _():
+        a1_copy(0).start()
+
     for h in range(2):
         for way in range(2):
             x_copy(1, h, way).start()
 
     def st_copy(d):
         k = add(tp, d, 16)
-        return remote(st_ref.at[k], strecv.at[tp], sts.at[d], strs.at[tp], at_tp(k))
+        return remote(st_ref.at[k], strecv.at[tp], sts.at[0], strs.at[0], at_tp(k))
 
     for copy in in_copies[5:]:
         copy.wait()
     fill_stats(h_ref, bq_ref, bk_ref, bv_ref, st_ref)
     for d in range(1, 16):
         st_copy(d).start()
-    a1[y] = w_ref[y]
+
+    @pl.when(at_home)
+    def _():
+        wz[own_j, x, yl, c] = w_ref[y]
+
     xg[y] = h_ref[...]
     strecv[tp] = st_ref[tp]
     turns(len_ref, rope)
 
-    for d in range(1, 8):
-        k = add(y, d, 8)
-        remote(a1.at[k], a1.at[k], a1s.at[d], a1r.at[k], at_y(k)).wait_recv()
-
-    own_j = (z // 4) * 2 + lax.rem(z, 2)
-
-    def a2_copy(d):
-        k = add(x, d, 4)
-        return remote(
-            a1.at[pl.ds(2 * k, 2)],
-            wz.at[own_j, x, :, c],
-            a2s.at[d],
-            a2r.at[x * 2 + c],
-            {"x": k, "c": zb},
-        )
-
-    for d in (2, 1, 3):
-        a2_copy(d).start()
-
-    @pl.when(zb != c)
-    def _():
-        a2_copy(0).start()
-
-    @pl.when(zb == c)
-    def _():
-        wz[own_j, x, :, c] = a1[pl.ds(2 * x, 2)]
-
-    x_step(1, 0)
-    x_step(1, 1)
 
     @pl.when(zb == c)
     def _():
         for q in range(4):
             kx = add(x, turn[q], 4)
-            for kc in (c, 1 - c):
-                if q == 0 and kc is c:
-                    continue
-                dst = wz.at[own_j, kx, :, kc]
-                k = kx * 2 + kc
-                remote(dst, dst, a2s.at[0], a2r.at[k], {"x": kx, "c": kc}).wait_recv()
+            for kl in range(2):
+                for kc in range(2):
+                    dst = wz.at[own_j, kx, kl, kc]
+                    k = kx * 4 + kl * 2 + kc
+
+                    @pl.when(jnp.logical_not(at_home & (k == tp)))
+                    def _(dst=dst, k=k, kx=kx, kc=kc):
+                        remote(dst, dst, a1s.at[0], a1r.at[k], {"x": kx, "c": 1 - c}).wait_recv()
+
             for way in range(2):
                 w_copy(1, q, way)[1].start()
 
-    x_step(2, 0)
-    x_step(2, 1)
-    for s in range(1, 5):
-        for q in range(4):
-            for way in range(2):
-                if goes_w(s, q, way):
-                    w_step(s, q, way)
-        if s <= 2:
-            x_step(s + 2, 0)
-            x_step(s + 2, 1)
-
-    def one_block(b, carry):
-        total = jnp.zeros((BR, COLS), jnp.float32)
-        for k in range(2):
-            total += jnp.dot(
-                xg[b * 2 + k],
-                wz[2 * k : 2 * k + 2].reshape(KB, COLS),
+    za, zl = z // 4, lax.rem(z, 2)
+    held = zb == c
+    far = jnp.where(zb == zl, za, 1 - za)
+    parts = (
+        jnp.where(held, 2 * za + zl, 2 * (1 - far) + 1 - zl),
+        jnp.where(held, 2 * za + 1 - zl, zl),
+        jnp.where(held, 2 * (1 - za) + 1 - zl, 2 + zl),
+        jnp.where(held, 2 * (1 - za) + zl, 2 * far + 1 - zl),
+    )
+
+    def product(b, which):
+        total = None
+        for n in which:
+            j = parts[n]
+            cols = pl.ds(pl.multiple_of(lax.rem(j, 2) * 256, 256), 256)
+            term = jnp.dot(
+                xg[b * 2 + j // 2, :, cols],
+                wz[j].reshape(256, COLS),
                 preferred_element_type=jnp.float32,
             )
-        acc[b] = total
+            total = term if total is None else total + term
+        return total
+
+    def rest(b, carry):
+        acc[b] += product(b, (2, 3))
         return carry
+
+    def w_both(s, q):
+        for way in range(2):
+            if goes_w(s, q, way):
+                w_step(s, q, way)
+
+    def first(d):
+        b = add(yh, d, 4)
+        acc[b] = product(b, (0, 1))
+
+    for kind, s, k in (
+        ("x", 1, 0), ("x", 1, 1), ("w", 1, 0), ("w", 1, 1), ("w", 1, 2), ("x", 2, 0), ("w", 1, 3),
+        ("w", 2, 0), ("x", 2, 1), ("w", 2, 1), ("w", 2, 2), ("x", 3, 0), ("w", 2, 3), ("w", 3, 0),
+        ("x", 3, 1), ("w", 3, 1), ("m", 0, 0), ("w", 3, 2), ("m", 0, 1), ("w", 3, 3), ("m", 0, 3),
+        ("x", 4, 0), ("x", 4, 1), ("m", 0, 2), ("w", 4, 0), ("w", 4, 1), ("w", 4, 2), ("w", 4, 3),
+    ):
+        if kind == "x":
+            x_step(s, k)
+        elif kind == "w":
+            w_both(s, k)
+        else:
+            first(k)
 
     oc = 1 - c
     HR = RT // 2
@@ -394,7 +435,7 @@
         )
 
     for half in range(2):
-        lax.fori_loop(2 * half, 2 * half + 2, one_block, 0)
+        lax.fori_loop(2 * half, 2 * half + 2, rest, 0)
         for d in order:
             dsend[half, d] = rows_for(half, add(x, d, 4), oc).astype(jnp.bfloat16)
             d_copy(half, d).start()
@@ -419,6 +460,26 @@
         r_copy(1, half).start()
     for half in range(2):
         fin[pl.ds(half * HR, HR), :] = both_cores(half, 1 if half == 0 else 3)
+    for d in range(1, 8):
+        a1_copy(d).wait_send()
+    sent = st_ref.at[pl.ds(0, 15)]
+    remote(sent, sent, sts.at[0], strs.at[0], at_tp(add(tp, 1, 16))).wait_send()
+
+    @pl.when(jnp.logical_not(at_home))
+    def _():
+        a1_copy(0).wait_send()
+
+    seven = xg.at[pl.ds(0, 7)]
+    remote(seven, seven, xs.at[0], xr.at[0, 0, 0], y_next[0]).wait_send()
+    for s in range(1, 5):
+        for q in range(4):
+            for way in range(2):
+                if goes_w(s, q, way):
+                    mine, copy = w_copy(s, q, way)
+
+                    @pl.when(mine)
+                    def _(copy=copy):
+                        copy.wait_send()
     for half in range(2):
         r_copy(0, half).wait_recv()
         total = fin[pl.ds(half * HR, HR), :] + rrecv[0, half].astype(jnp.float32)
@@ -465,61 +526,48 @@
     def _():
         yrecv[y] = ysend[yh, c]
 
-    for d in range(1, 16):
-        k = add(tp, d, 16)
-        remote(strecv.at[k], strecv.at[k], sts.at[d], strs.at[k], at_tp(k)).wait_recv()
+    fifteen = strecv.at[pl.ds(0, 15)]
+    remote(fifteen, fifteen, sts.at[0], strs.at[0], at_tp(add(tp, 1, 16))).wait_recv()
     for copy in pool_copies:
         copy.wait()
-
-    inv = row_scale(strecv)
-
-    def one_group(d, carry):
-        kh = lax.rem(yh + jnp.where(d == 2, 3, jnp.where(d == 3, 2, d)), 4)
-        for i in range(2):
-            k = kh * 2 + i
-
-            @pl.when((k != y) | (yl != c))
-            def _(k=k):
-                remote(
-                    yrecv.at[k], yrecv.at[k], yss.at[1, 0], yrs.at[k], {"yh": add(yh, 1, 4)}
-                ).wait_recv()
-
-        attend(kh, inv, len_ref, table_ref, yrecv, strecv, rope, kpool, vpool, out_ref)
-        return carry
-
-    lax.fori_loop(0, 4, one_group, 0)
-
-    for d in range(1, 8):
-        a1_copy(d).wait_send()
-    y_each(lambda copy: copy.wait_send())
-    for d in range(1, 16):
-        st_copy(d).wait_send()
-    for d in range(1, 4):
-        a2_copy(d).wait_send()
-
-    @pl.when(zb != c)
-    def _():
-        a2_copy(0).wait_send()
 
     for half in range(2):
         for d in range(4):
             d_copy(half, d).wait_send()
         for kind in range(3):
             r_copy(kind, half).wait_send()
-    for s in range(1, 5):
-        for h in range(2):
-            for way in range(2):
-                if goes(s, h, way):
-                    x_copy(s, h, way).wait_send()
-    for s in range(1, 5):
-        for q in range(4):
-            for way in range(2):
-                if goes_w(s, q, way):
-                    mine, copy = w_copy(s, q, way)
-
-                    @pl.when(mine)
-                    def _(copy=copy):
-                        copy.wait_send()
+    inv = row_scale(strecv)
+
+    def out_copy(d):
+        kh = lax.rem(yh + jnp.where(d == 2, 3, jnp.where(d == 3, 2, d)), 4)
+        at = pl.ds(pl.multiple_of(kh * GROUP * HD, GROUP * HD), GROUP * HD)
+        return kh, pltpu.make_async_copy(
+            out_ref.at[:, :, at], out_hbm.at[:, :, at], outs.at[d]
+        )
+
+    def one_pair(p, carry):
+        groups = []
+        for u in range(2):
+            kh, _ = out_copy(2 * p + u)
+            groups.append(kh)
+            for i in range(2):
+                k = kh * 2 + i
+
+                @pl.when((k != y) | (yl != c))
+                def _(k=k):
+                    remote(
+                        yrecv.at[k], yrecv.at[k], yss.at[1, 0], yrs.at[k], {"yh": add(yh, 1, 4)}
+                    ).wait_recv()
+
+        attend(groups, inv, len_ref, table_ref, yrecv, strecv, rope, kpool, vpool, score, out_ref)
+        for u in range(2):
+            out_copy(2 * p + u)[1].start()
+        return carry
+
+    lax.fori_loop(0, 2, one_pair, 0)
+    y_each(lambda copy: copy.wait_send())
+    for d in range(4):
+        out_copy(d)[1].wait()
 
 
 def on_device(
@@ -542,11 +590,14 @@
     f32 = jnp.float32
     out = pl.pallas_call(
         step_kernel,
-        out_shape=jax.ShapeDtypeStruct((ROWS, STEPS, HQ * HD), f32),
-        in_specs=[pl.BlockSpec(memory_space=pltpu.SMEM)] * 2
-        + [pl.BlockSpec(memory_space=pl.ANY)] * 10,
-        out_specs=pl.BlockSpec(memory_space=vm),
+        out_shape=jax.ShapeDtypeStruct((ROWS, STEPS, HQ * HD), bf),
+        in_specs=[pl.BlockSpec(memory_space=pl.ANY)] * 12,
+        out_specs=pl.BlockSpec(memory_space=pl.ANY),
         scratch_shapes=[
+            pltpu.SMEM((ROWS,), jnp.int32),
+            pltpu.SMEM((ROWS, MOSTP), jnp.int32),
+            vm((ROWS, STEPS, HQ * HD), bf),
+            vm((2 * ROWS, GROUP * STEPS, KEYS), f32),
             vm((ROWS * 16, STEPS, KB), bf),
             vm((D // 128, 128), f32),
             vm((16, HQ * HD), f32),
@@ -562,7 +613,6 @@
             vm((16, KVH, PAGE, HD), bf),
             vm((16, KVH, PAGE, HD), bf),
             vm((8, BR, KB), bf),
-            vm((8, 16, COLS), bf),
             vm((4, 4, 2, 2, 16, COLS), bf),
             vm((4, BR, COLS), f32),
             vm((2, 4, RT // 2, COLS), bf),
@@ -573,12 +623,11 @@
             vm((4, 2, 16, COLS), bf),
             vm((8, 16, COLS), bf),
             vm((16, 8, 128), f32),
-            dma((8,)), dma((2,)),
-            dma((2, 4, 2)), dma((2, 4, 2)),
-            dma((8,)), dma((8,)),
-            dma((4,)), dma((8,)),
+            dma((10,)), dma((4,)), dma((2,)),
+            dma((1,)), dma((2, 4, 2)),
+            dma((8,)), dma((16,)),
             dma((2, 4, 4)), dma((2, 4, 4)),
-            dma((16,)), dma((16,)),
+            dma((1,)), dma((1,)),
             dma((2, 4)), dma((2, 4)),
             dma((3, 2)), dma((3, 2)),
             dma((4, 2)), dma((8,)),
@@ -599,7 +648,7 @@
         key_pages,
         value_pages,
     )
-    return out.astype(bf)
+    return out
 
 
 def solution(mesh):

time: 70 us -> 61.4 us (0.88)
  Pallas kernels: 68.3 us -> 59.3 us
  other arithmetic: 1.6 us -> 0 us
  local copies, waits for them, and re-layouts: 0 us -> 1.57 us
    pallas_call x1, Pallas kernels: 68.3 us -> 59.3 us  [on_device(): pl.pallas_call(step_kernel, out_shape=jax.ShapeDtypeStruct((ROWS, STEPS,...]
    convert_element_type x1 -> x0, other arithmetic: 1.6 us -> none  [on_device(): return out.astype(bf)]
    unnamed x0 -> x1, local copies, waits for them, and re-layouts: none -> 1.57 us
where the time goes in v4:
time: 61.4 us; the launch traced here: 60.8 us
  Pallas kernels  59.3 us (97%)
  local copies, waits for them, and re-layouts  1.57 us (3%)
    pallas_call x1, Pallas kernels, on_device(): pl.pallas_call(step_kernel, out_shape=jax.ShapeDtypeStruct((ROWS, STEPS,...  59.3 us
    unnamed x1, local copies, waits for them, and re-layouts  1.57 us

profile of v4, /device:TPU:1, one launch (start us, length us, event | category | flops | bytes accessed | tf_op | source)
XLA Modules:
  0.0 60.8 jit_solution(5983443690569950256)
XLA Ops:
  0.0 59.3 %step.1 = bf16[3,4,4096]{2,1,0:T(4,128)(2,1)} custom-call(s32[3]{0:T(128)} %len_hbm.1, s32[3,8]{1,0:T(4,128)} %table_hbm.1, bf16[48,4,512]{2,1,0:T(4,128)(2,1)} %h_hbm.1, f32[64,128]{1,0:T(8,128)} %bitcast.4, f32[16,4096]{1,0:T(8,128)} %wq_hbm.1, f32[16,512]{1,0:T(8,128)} %wk_hbm.1, f32[16,512]{1,0:T(8,128)} %wv_hbm.1, f32[2,128]{1,0:T(2,128)} %bitcast.5, ...), custom_call_target="tpu_custom_call" | custom-call | tf_op jit(solution)/shard_map/step/pallas_call | solution.py:591
  59.3 1.6 %copy.14 = bf16[3,4,4096]{2,1,0:T(4,128)(2,1)} copy(bf16[3,4,4096]{2,1,0:T(4,128)(2,1)} %step.1) | data formatting | bytes 196608

commit v5 on v4

--- a/solution.py
+++ b/solution.py
@@ -288,25 +288,26 @@
 
     def w_copy(s, q, way):
         _, mine, j = origin_w(s - 1, way)
-        part = wz.at[j, add(x, turn[q], 4)]
+        part = wz.at[j * 4 + add(x, turn[q], 4)]
         return mine, remote(
-            part, part, ws.at[way, s - 1, q], wr.at[way, s - 1, q], z_next[way]
+            part, part, ws.at[0], wr.at[way, s - 1, q], z_next[way]
         )
 
     def w_step(s, q, way):
         _, mine, j = origin_w(s, way)
-        part = wz.at[j, add(x, turn[q], 4)]
+        part = wz.at[j * 4 + add(x, turn[q], 4)]
 
         @pl.when(mine)
         def _():
             remote(
-                part, part, ws.at[way, s - 1, q], wr.at[way, s - 1, q], z_next[way]
+                part, part, ws.at[0], wr.at[way, s - 1, q], z_next[way]
             ).wait_recv()
             if goes_w(s + 1, q, way):
                 w_copy(s + 1, q, way)[1].start()
 
-    def x_step(s, h):
+    def x_step(s, n):
         for way in range(2):
+            h = n ^ way
             if goes(s, h, way):
                 x_wait(s, h, way)
                 if goes(s + 1, h, way):
@@ -318,13 +319,14 @@
         k = add(y, d, 8)
         return remote(
             w_ref.at[k],
-            wz.at[own_j, x, yl, c],
-            a1s.at[d],
-            a1r.at[tp],
+            wz.at[own_j * 4 + x, yl, c],
+            a1s.at[0 if d else 1],
+            a1r.at[x],
             {"x": yh, "yh": k // 2, "yl": lax.rem(k, 2), "c": zb},
         )
 
-    at_home = (x == yh) & (zb == c)
+    held = zb == c
+    at_home = (x == yh) & held
     for d in (4, 3, 5, 2, 6, 1, 7):
         a1_copy(d).start()
 
@@ -334,7 +336,7 @@
 
     for h in range(2):
         for way in range(2):
-            x_copy(1, h, way).start()
+            x_copy(1, h ^ way, way).start()
 
     def st_copy(d):
         k = add(tp, d, 16)
@@ -348,31 +350,37 @@
 
     @pl.when(at_home)
     def _():
-        wz[own_j, x, yl, c] = w_ref[y]
+        wz[own_j * 4 + x, yl, c] = w_ref[y]
 
     xg[y] = h_ref[...]
     strecv[tp] = st_ref[tp]
     turns(len_ref, rope)
 
 
-    @pl.when(zb == c)
+    @pl.when(held)
     def _():
-        for q in range(4):
+        for q in (0, 2, 1, 3):
             kx = add(x, turn[q], 4)
-            for kl in range(2):
-                for kc in range(2):
-                    dst = wz.at[own_j, kx, kl, kc]
-                    k = kx * 4 + kl * 2 + kc
-
-                    @pl.when(jnp.logical_not(at_home & (k == tp)))
-                    def _(dst=dst, k=k, kx=kx, kc=kc):
-                        remote(dst, dst, a1s.at[0], a1r.at[k], {"x": kx, "c": 1 - c}).wait_recv()
-
+            if q == 0:
+
+                @pl.when(at_home)
+                def _():
+                    three = w_ref.at[pl.ds(0, 3)]
+                    remote(three, three, a1s.at[0], a1r.at[x], {"c": 1 - c}).wait_recv()
+
+                @pl.when(jnp.logical_not(at_home))
+                def _():
+                    four = wz.at[own_j * 4 + x]
+                    remote(four, four, a1s.at[0], a1r.at[x], {"c": 1 - c}).wait_recv()
+            else:
+                four = wz.at[own_j * 4 + kx]
+                remote(four, four, a1s.at[0], a1r.at[kx], {"x": kx}).wait_recv()
+            w_copy(1, q, q // 2)[1].start()
+        for n in range(2):
             for way in range(2):
-                w_copy(1, q, way)[1].start()
+                w_copy(1, (n + 2 - 2 * way), way)[1].start()
 
     za, zl = z // 4, lax.rem(z, 2)
-    held = zb == c
     far = jnp.where(zb == zl, za, 1 - za)
     parts = (
         jnp.where(held, 2 * za + zl, 2 * (1 - far) + 1 - zl),
@@ -388,7 +396,7 @@
             cols = pl.ds(pl.multiple_of(lax.rem(j, 2) * 256, 256), 256)
             term = jnp.dot(
                 xg[b * 2 + j // 2, :, cols],
-                wz[j].reshape(256, COLS),
+                wz[pl.ds(4 * j, 4)].reshape(256, COLS),
                 preferred_element_type=jnp.float32,
             )
             total = term if total is None else total + term
@@ -398,8 +406,9 @@
         acc[b] += product(b, (2, 3))
         return carry
 
-    def w_both(s, q):
+    def w_both(s, n):
         for way in range(2):
+            q = (n + 2 * way) % 4
             if goes_w(s, q, way):
                 w_step(s, q, way)
 
@@ -409,9 +418,9 @@
 
     for kind, s, k in (
         ("x", 1, 0), ("x", 1, 1), ("w", 1, 0), ("w", 1, 1), ("w", 1, 2), ("x", 2, 0), ("w", 1, 3),
-        ("w", 2, 0), ("x", 2, 1), ("w", 2, 1), ("w", 2, 2), ("x", 3, 0), ("w", 2, 3), ("w", 3, 0),
-        ("x", 3, 1), ("w", 3, 1), ("m", 0, 0), ("w", 3, 2), ("m", 0, 1), ("w", 3, 3), ("m", 0, 3),
-        ("x", 4, 0), ("x", 4, 1), ("m", 0, 2), ("w", 4, 0), ("w", 4, 1), ("w", 4, 2), ("w", 4, 3),
+        ("w", 2, 0), ("w", 2, 1), ("x", 2, 1), ("w", 2, 2), ("w", 2, 3), ("x", 3, 0), ("w", 3, 0),
+        ("w", 3, 1), ("x", 3, 1), ("m", 0, 0), ("w", 3, 2), ("m", 0, 1), ("w", 3, 3), ("m", 0, 3),
+        ("x", 4, 0), ("m", 0, 2), ("w", 4, 0), ("w", 4, 1),
     ):
         if kind == "x":
             x_step(s, k)
@@ -431,7 +440,7 @@
 
     def d_copy(half, d):
         return remote(
-            dsend.at[half, d], drecv.at[half, d], d2s.at[half, d], d2r.at[half, d], {"c": oc}
+            dsend.at[half, d], drecv.at[half, d], d2s.at[0], d2r.at[half, d], {"c": oc}
         )
 
     for half in range(2):
@@ -446,22 +455,27 @@
 
     x_next = ({"x": add(x, 1, 4)}, {"x": add(x, -1, 4)})
 
-    def r_copy(kind, half):
-        way = half if kind == 0 else (1 - half if kind == 1 else half)
+    def r_copy(kind, half, u):
+        way = 1 - half if kind == 1 else half
         return remote(
-            rsend.at[kind, half], rrecv.at[kind, half], rss.at[kind, half], rrs.at[kind, half],
+            rsend.at[kind, half, u], rrecv.at[kind, half, u], rss.at[0], rrs.at[kind, half, u],
             x_next[way],
         )
 
+    def send_half(kind, half, d):
+        total = both_cores(half, d).astype(jnp.bfloat16)
+        for u in range(2):
+            rsend[kind, half, u] = total[24 * u : 24 * u + 24]
+            r_copy(kind, half, u).start()
+
     for half in range(2):
-        rsend[0, half] = both_cores(half, 2).astype(jnp.bfloat16)
-        r_copy(0, half).start()
-        rsend[1, half] = both_cores(half, 3 if half == 0 else 1).astype(jnp.bfloat16)
-        r_copy(1, half).start()
+        send_half(0, half, 2)
+    for half in range(2):
+        send_half(1, half, 3 if half == 0 else 1)
     for half in range(2):
         fin[pl.ds(half * HR, HR), :] = both_cores(half, 1 if half == 0 else 3)
-    for d in range(1, 8):
-        a1_copy(d).wait_send()
+    some = w_ref.at[pl.ds(0, 7)]
+    remote(some, some, a1s.at[0], a1r.at[0], y_next[0]).wait_send()
     sent = st_ref.at[pl.ds(0, 15)]
     remote(sent, sent, sts.at[0], strs.at[0], at_tp(add(tp, 1, 16))).wait_send()
 
@@ -471,29 +485,26 @@
 
     seven = xg.at[pl.ds(0, 7)]
     remote(seven, seven, xs.at[0], xr.at[0, 0, 0], y_next[0]).wait_send()
-    for s in range(1, 5):
-        for q in range(4):
-            for way in range(2):
-                if goes_w(s, q, way):
-                    mine, copy = w_copy(s, q, way)
-
-                    @pl.when(mine)
-                    def _(copy=copy):
-                        copy.wait_send()
-    for half in range(2):
-        r_copy(0, half).wait_recv()
-        total = fin[pl.ds(half * HR, HR), :] + rrecv[0, half].astype(jnp.float32)
-        rsend[2, half] = total.astype(jnp.bfloat16)
-        r_copy(2, half).start()
+    most = wz.at[pl.ds(0, 14)]
+    remote(most, most, ws.at[0], wr.at[0, 0, 0], z_next[0]).wait_send()
+
+    def part_rows(half, u):
+        return pl.ds(half * HR + 24 * u, 24)
+
+    for u in range(2):
+        for half in range(2):
+            r_copy(0, half, u).wait_recv()
+            total = fin[part_rows(half, u), :] + rrecv[0, half, u].astype(jnp.float32)
+            rsend[2, half, u] = total.astype(jnp.bfloat16)
+            r_copy(2, half, u).start()
     fin[pl.ds(RT, 8), :] = jnp.zeros((8, COLS), jnp.float32)
     for half in range(2):
         fin[pl.ds(half * HR, HR), :] = both_cores(half, 0)
-    for half in range(2):
-        r_copy(1, half).wait_recv()
-        fin[pl.ds(half * HR, HR), :] += rrecv[1, half].astype(jnp.float32)
-    for half in range(2):
-        r_copy(2, half).wait_recv()
-        fin[pl.ds(half * HR, HR), :] += rrecv[2, half].astype(jnp.float32)
+    for kind in (1, 2):
+        for u in range(2):
+            for half in range(2):
+                r_copy(kind, half, u).wait_recv()
+                fin[part_rows(half, u), :] += rrecv[kind, half, u].astype(jnp.float32)
 
     def y_copy(d, dc):
         k = add(yh, d, 4)
@@ -501,7 +512,7 @@
         return remote(
             ysend.at[k, kc],
             yrecv.at[y],
-            yss.at[d, dc],
+            yss.at[0 if d or dc else 1],
             yrs.at[y],
             {"yh": k, "yl": c, "c": kc},
         )
@@ -531,11 +542,8 @@
     for copy in pool_copies:
         copy.wait()
 
-    for half in range(2):
-        for d in range(4):
-            d_copy(half, d).wait_send()
-        for kind in range(3):
-            r_copy(kind, half).wait_send()
+    remote(dsend, dsend, d2s.at[0], d2r.at[0, 0], {"c": oc}).wait_send()
+    remote(rsend, rsend, rss.at[0], rrs.at[0, 0, 0], x_next[0]).wait_send()
     inv = row_scale(strecv)
 
     def out_copy(d):
@@ -556,7 +564,7 @@
                 @pl.when((k != y) | (yl != c))
                 def _(k=k):
                     remote(
-                        yrecv.at[k], yrecv.at[k], yss.at[1, 0], yrs.at[k], {"yh": add(yh, 1, 4)}
+                        yrecv.at[k], yrecv.at[k], yss.at[0], yrs.at[k], {"yh": add(yh, 1, 4)}
                     ).wait_recv()
 
         attend(groups, inv, len_ref, table_ref, yrecv, strecv, rope, kpool, vpool, score, out_ref)
@@ -565,7 +573,13 @@
         return carry
 
     lax.fori_loop(0, 2, one_pair, 0)
-    y_each(lambda copy: copy.wait_send())
+    rest_of = yrecv.at[pl.ds(0, 7)]
+    remote(rest_of, rest_of, yss.at[0], yrs.at[0], y_next[0]).wait_send()
+
+    @pl.when(yl != c)
+    def _():
+        y_copy(0, 0).wait_send()
+
     for d in range(4):
         out_copy(d)[1].wait()
 
@@ -613,24 +627,24 @@
             vm((16, KVH, PAGE, HD), bf),
             vm((16, KVH, PAGE, HD), bf),
             vm((8, BR, KB), bf),
-            vm((4, 4, 2, 2, 16, COLS), bf),
+            vm((16, 2, 2, 16, COLS), bf),
             vm((4, BR, COLS), f32),
             vm((2, 4, RT // 2, COLS), bf),
             vm((2, 4, RT // 2, COLS), bf),
-            vm((3, 2, RT // 2, COLS), bf),
-            vm((3, 2, RT // 2, COLS), bf),
+            vm((3, 2, 2, 24, COLS), bf),
+            vm((3, 2, 2, 24, COLS), bf),
             vm((RT + 8, COLS), f32),
             vm((4, 2, 16, COLS), bf),
             vm((8, 16, COLS), bf),
             vm((16, 8, 128), f32),
             dma((10,)), dma((4,)), dma((2,)),
             dma((1,)), dma((2, 4, 2)),
-            dma((8,)), dma((16,)),
-            dma((2, 4, 4)), dma((2, 4, 4)),
+            dma((2,)), dma((4,)),
+            dma((1,)), dma((2, 4, 4)),
             dma((1,)), dma((1,)),
-            dma((2, 4)), dma((2, 4)),
-            dma((3, 2)), dma((3, 2)),
-            dma((4, 2)), dma((8,)),
+            dma((1,)), dma((2, 4)),
+            dma((1,)), dma((3, 2, 2)),
+            dma((2,)), dma((8,)),
         ],
         compiler_params=pltpu.CompilerParams(collective_id=0, has_side_effects=True),
         name="step",

time: 61.4 us -> 59.4 us (0.967)
  Pallas kernels: 59.3 us -> 57.6 us
    pallas_call x1, Pallas kernels: 59.3 us -> 57.6 us  [on_device(): pl.pallas_call(step_kernel, out_shape=jax.ShapeDtypeStruct((ROWS, STEPS,...]
where the time goes in v5:
time: 59.4 us; the launch traced here: 59.2 us
  Pallas kernels  57.6 us (97%)
  local copies, waits for them, and re-layouts  1.57 us (3%)
    pallas_call x1, Pallas kernels, on_device(): pl.pallas_call(step_kernel, out_shape=jax.ShapeDtypeStruct((ROWS, STEPS,...  57.6 us
    unnamed x1, local copies, waits for them, and re-layouts  1.57 us

profile of v5, /device:TPU:1, one launch (start us, length us, event | category | flops | bytes accessed | tf_op | source)
XLA Modules:
  0.0 59.2 jit_solution(1146636329839732376)
XLA Ops:
  0.0 57.6 %step.1 = bf16[3,4,4096]{2,1,0:T(4,128)(2,1)} custom-call(s32[3]{0:T(128)} %len_hbm.1, s32[3,8]{1,0:T(4,128)} %table_hbm.1, bf16[48,4,512]{2,1,0:T(4,128)(2,1)} %h_hbm.1, f32[64,128]{1,0:T(8,128)} %bitcast.4, f32[16,4096]{1,0:T(8,128)} %wq_hbm.1, f32[16,512]{1,0:T(8,128)} %wk_hbm.1, f32[16,512]{1,0:T(8,128)} %wv_hbm.1, f32[2,128]{1,0:T(2,128)} %bitcast.5, ...), custom_call_target="tpu_custom_call" | custom-call | tf_op jit(solution)/shard_map/step/pallas_call | solution.py:605
  57.6 1.6 %copy.14 = bf16[3,4,4096]{2,1,0:T(4,128)(2,1)} copy(bf16[3,4,4096]{2,1,0:T(4,128)(2,1)} %step.1) | data formatting | bytes 196608

commit v6 on v5

--- a/solution.py
+++ b/solution.py
@@ -140,11 +140,11 @@
         heads = []
         for g in range(GROUP):
             i, a = g // 4, g % 4
-            total = qkv[2 * kh + i, :, a * HD : (a + 1) * HD].astype(jnp.float32)
+            total = qkv[2 * kh + i, OWN * a : OWN * a + 16, :]
             bias = st[2 * (2 * kh + i) + a // 2, a % 2 : a % 2 + 1, :]
             heads.append(rotated(made(total, bias)))
-        t0 = qkv[2 * kh, :, 4 * HD : 5 * HD].astype(jnp.float32)
-        t1 = qkv[2 * kh + 1, :, 4 * HD : 5 * HD].astype(jnp.float32)
+        t0 = qkv[2 * kh, 4 * OWN : 4 * OWN + 16, :]
+        t1 = qkv[2 * kh + 1, 4 * OWN : 4 * OWN + 16, :]
         k_new = rotated(made(jnp.where(low, t0, pltpu.roll(t1, HD // 2, 1)), small_bias(kh, 2)))
         v_new = made(jnp.where(low, pltpu.roll(t0, HD // 2, 1), t1), small_bias(kh, 3))
         made_of.append((jnp.concatenate(heads, axis=0), k_new, v_new.astype(jnp.bfloat16)))
@@ -196,7 +196,7 @@
     out_hbm,
     len_ref, table_ref, out_ref, score, raw, gain_ref, wq_ref, wk_ref, wv_ref, bq_ref, bk_ref, bv_ref, h_ref,
     w_ref, st_ref, rope, kpool, vpool,
-    xg, wz, acc, dsend, drecv, rsend, rrecv, fin, ysend, yrecv, strecv,
+    xg, wz, acc, dsend, drecv, rsend, rrecv, fin, ysend, yrecv, packed, strecv,
     ins, outs, pools, xs, xr, a1s, a1r, ws, wr, sts, strs, d2s, d2r, rss, rrs, yss, yrs,
 ):
     yh, z, x, yl, c = (lax.axis_index(a) for a in AXES)
@@ -436,18 +436,10 @@
         at = pl.multiple_of((kx * 2 + kc) * 24, 8)
         return acc[2 * half : 2 * half + 2, pl.ds(at, 24), :].reshape(HR, COLS)
 
-    order = (2, 1, 3, 0)
-
     def d_copy(half, d):
         return remote(
             dsend.at[half, d], drecv.at[half, d], d2s.at[0], d2r.at[half, d], {"c": oc}
         )
-
-    for half in range(2):
-        lax.fori_loop(2 * half, 2 * half + 2, rest, 0)
-        for d in order:
-            dsend[half, d] = rows_for(half, add(x, d, 4), oc).astype(jnp.bfloat16)
-            d_copy(half, d).start()
 
     def both_cores(half, d):
         d_copy(half, d).wait_recv()
@@ -468,8 +460,21 @@
             rsend[kind, half, u] = total[24 * u : 24 * u + 24]
             r_copy(kind, half, u).start()
 
+    def d_send(half, d):
+        dsend[half, d] = rows_for(half, add(x, d, 4), oc).astype(jnp.bfloat16)
+        d_copy(half, d).start()
+
+    lax.fori_loop(0, 2, rest, 0)
+    d_send(0, 2)
+    lax.fori_loop(2, 4, rest, 0)
+    for half, d in ((1, 2), (0, 3), (1, 1)):
+        d_send(half, d)
+    send_half(0, 0, 2)
+    for half, d in ((0, 1), (1, 3)):
+        d_send(half, d)
+    send_half(0, 1, 2)
     for half in range(2):
-        send_half(0, half, 2)
+        d_send(half, 0)
     for half in range(2):
         send_half(1, half, 3 if half == 0 else 1)
     for half in range(2):
@@ -530,7 +535,11 @@
 
     for k in range(4):
         for kc in range(2):
-            ysend[k, kc] = fin[pl.ds(24 * k + OWN * kc, 16), :].astype(jnp.bfloat16)
+            for t in range(COLS // HD):
+                packed[k * 2 + kc, OWN * t : OWN * (t + 1), :] = fin[
+                    pl.ds(24 * k + OWN * kc, OWN), HD * t : HD * (t + 1)
+                ]
+            ysend[k, kc] = packed[k * 2 + kc].astype(jnp.bfloat16)
     y_each(lambda copy: copy.start())
 
     @pl.when(yl == c)
@@ -567,7 +576,10 @@
                         yrecv.at[k], yrecv.at[k], yss.at[0], yrs.at[k], {"yh": add(yh, 1, 4)}
                     ).wait_recv()
 
-        attend(groups, inv, len_ref, table_ref, yrecv, strecv, rope, kpool, vpool, score, out_ref)
+        for kh in groups:
+            for i in range(2):
+                packed[kh * 2 + i] = yrecv[kh * 2 + i].astype(jnp.float32)
+        attend(groups, inv, len_ref, table_ref, packed, strecv, rope, kpool, vpool, score, out_ref)
         for u in range(2):
             out_copy(2 * p + u)[1].start()
         return carry
@@ -634,8 +646,9 @@
             vm((3, 2, 2, 24, COLS), bf),
             vm((3, 2, 2, 24, COLS), bf),
             vm((RT + 8, COLS), f32),
-            vm((4, 2, 16, COLS), bf),
-            vm((8, 16, COLS), bf),
+            vm((4, 2, 64, HD), bf),
+            vm((8, 64, HD), bf),
+            vm((8, 64, HD), f32),
             vm((16, 8, 128), f32),
             dma((10,)), dma((4,)), dma((2,)),
             dma((1,)), dma((2, 4, 2)),

time: 59.4 us -> 58.8 us (0.990)
  no operation moved by 1% of the time
where the time goes in v6:
time: 58.8 us; the launch traced here: 58.6 us
  Pallas kernels  57.1 us (97%)
  local copies, waits for them, and re-layouts  1.57 us (3%)
    pallas_call x1, Pallas kernels, on_device(): pl.pallas_call(step_kernel, out_shape=jax.ShapeDtypeStruct((ROWS, STEPS,...  57.1 us
    unnamed x1, local copies, waits for them, and re-layouts  1.57 us

profile of v6, /device:TPU:1, one launch (start us, length us, event | category | flops | bytes accessed | tf_op | source)
XLA Modules:
  0.0 58.6 jit_solution(5642565778349390856)
XLA Ops:
  0.0 57.1 %step.1 = bf16[3,4,4096]{2,1,0:T(4,128)(2,1)} custom-call(s32[3]{0:T(128)} %len_hbm.1, s32[3,8]{1,0:T(4,128)} %table_hbm.1, bf16[48,4,512]{2,1,0:T(4,128)(2,1)} %h_hbm.1, f32[64,128]{1,0:T(8,128)} %bitcast.4, f32[16,4096]{1,0:T(8,128)} %wq_hbm.1, f32[16,512]{1,0:T(8,128)} %wk_hbm.1, f32[16,512]{1,0:T(8,128)} %wv_hbm.1, f32[2,128]{1,0:T(2,128)} %bitcast.5, ...), custom_call_target="tpu_custom_call" | custom-call | tf_op jit(solution)/shard_map/step/pallas_call | solution.py:617
  57.1 1.6 %copy.14 = bf16[3,4,4096]{2,1,0:T(4,128)(2,1)} copy(bf16[3,4,4096]{2,1,0:T(4,128)(2,1)} %step.1) | data formatting | bytes 196608
